TPU v7x, 128 devices: a whole 4x4x4 slice. The times are simulated.
128 devices in a mesh: expert: 128 (over y, x, z, core).
Axes of the slice: x: 4, y: 4, z: 4, core: 2. Of those that a mesh axis runs over, the one named last changes fastest.
Arguments:
- tokens: bfloat16 [16384, 4096], P('expert'), may hold values from -6 to 6
- norm_gain: float32 [4096], replicated, may hold values from 0.5 to 1.5
- router_weight: bfloat16 [4096, 128], replicated, may hold values from -0.09375 to 0.09375
- expert_ids: int32 [16384, 2], P('expert'), may hold values from 0 to 127, as said below
- gate_proj: bfloat16 [128, 4096, 768], P('expert'), may hold values from -0.09375 to 0.09375
- up_proj: bfloat16 [128, 4096, 768], P('expert'), may hold values from -0.09375 to 0.09375
- down_proj: bfloat16 [128, 768, 4096], P('expert'), may hold values from -0.21875 to 0.21875
- value_weight: bfloat16 [4096], replicated, may hold values from -0.09375 to 0.09375
- value_target: int32 [16384], P('expert'), may hold values from -1 to 1
- recency: float32 [16384], P('expert'), may hold values from 0.25 to 18, as said below
Outputs:
- mixed: bfloat16 [16384, 4096], P('expert')
- values: float32 [16384], P('expert')
- loss: float32 [], replicated
Inputs may be any that keep to these rules, and one draw needn't show every extreme that they name: `expert_ids`: each row names two different experts; among the rows of one device no expert is named more than 3 times. `recency`: positive weights.
All inputs are finite; a program needn't handle non-finite values.
Results may differ from a plain program's by a relative error of at most 0.0055.
Values may be sent and summed in bfloat16 or wider, within the bound.
No kernel may reach another device: no remote copies, remote signals or barrier semaphores. Data moves between devices by JAX's collectives and lax.ppermute only.
A program may use at most 128 MiB of HBM per device.

v0:
```python
import jax
import jax.numpy as jnp
from jax import lax
from jax.sharding import Mesh
from jax.sharding import PartitionSpec as P

EXPERT = ("expert_0", "expert_1", "expert_2", "expert_3")


def by_axis(x, axes):
    for axis in axes:
        x = lax.psum(x, axis)
    return x


def expert_ffn(received, gate_proj, up_proj, down_proj):
    sources, slots, width = received.shape
    flat_input = received.reshape(sources * slots, width)
    gate_part = jnp.dot(flat_input, gate_proj[0], preferred_element_type=jnp.float32)
    up_part = jnp.dot(flat_input, up_proj[0], preferred_element_type=jnp.float32)
    hidden = (jax.nn.silu(gate_part) * up_part).astype(jnp.bfloat16)
    result = jnp.dot(hidden, down_proj[0], preferred_element_type=jnp.float32).astype(jnp.bfloat16)
    return result.reshape(sources, slots, width)


def body(
    tokens,
    norm_gain,
    router_weight,
    expert_ids,
    gate_proj,
    up_proj,
    down_proj,
    value_weight,
    value_target,
    recency,
):
    token_count, width = tokens.shape
    expert_total = router_weight.shape[1]
    capacity = 3 * token_count // expert_total
    wide = tokens.astype(jnp.float32)
    inverse = lax.rsqrt(jnp.mean(wide * wide, axis=1, keepdims=True) + 1e-05)
    normed = (wide * inverse * norm_gain).astype(jnp.bfloat16)
    logits = jnp.dot(normed, router_weight, preferred_element_type=jnp.float32)
    columns = lax.broadcasted_iota(jnp.int32, (1, expert_total), 1)
    first = jnp.sum(jnp.where(expert_ids[:, 0:1] == columns, logits, 0.0), axis=1)
    second = jnp.sum(jnp.where(expert_ids[:, 1:2] == columns, logits, 0.0), axis=1)
    gate_first = jax.nn.sigmoid(first - second)
    gate_second = jax.nn.sigmoid(second - first)
    flat_ids = expert_ids.reshape(-1)
    one_hot = (flat_ids[:, None] == columns).astype(jnp.int32)
    slot_rank = jnp.sum(jnp.cumsum(one_hot, axis=0) * one_hot, axis=1) - 1
    slot_index = flat_ids * capacity + slot_rank
    row_index = jnp.arange(2 * token_count, dtype=jnp.int32) // 2
    source_row = (
        jnp.full((expert_total * capacity,), token_count, dtype=jnp.int32)
        .at[slot_index]
        .set(row_index)
    )
    padded = jnp.concatenate([normed, jnp.zeros((1, width), jnp.bfloat16)], axis=0)
    outgoing = padded[source_row].reshape(expert_total, capacity, width)
    received = lax.all_to_all(outgoing, EXPERT, split_axis=0, concat_axis=0, tiled=True)
    produced = expert_ffn(received, gate_proj, up_proj, down_proj)
    returned = lax.all_to_all(produced, EXPERT, split_axis=0, concat_axis=0, tiled=True)
    flat_back = returned.reshape(expert_total * capacity, width)
    picked = flat_back[slot_index].reshape(token_count, 2, width)
    mixed = (
        wide
        + gate_first[:, None] * picked[:, 0].astype(jnp.float32)
        + gate_second[:, None] * picked[:, 1].astype(jnp.float32)
    ).astype(jnp.bfloat16)
    values = jnp.tanh(jnp.dot(mixed, value_weight, preferred_element_type=jnp.float32))
    error = values - value_target.astype(jnp.float32)
    weighted, weight_total = (
        by_axis(jnp.sum(recency * error * error), EXPERT),
        by_axis(jnp.sum(recency), EXPERT),
    )
    loss = weighted / weight_total
    return (mixed, values, loss)


def solution(mesh):
    finer = Mesh(mesh.devices.reshape(4, 4, 4, 2), ("expert_0", "expert_1", "expert_2", "expert_3"))
    in_specs = (
        P(EXPERT, None),
        P(),
        P(),
        P(EXPERT, None),
        P(EXPERT, None, None),
        P(EXPERT, None, None),
        P(EXPERT, None, None),
        P(),
        P(EXPERT),
        P(EXPERT),
    )
    out_specs = (P(EXPERT, None), P(EXPERT), P())
    return jax.shard_map(body, mesh=finer, in_specs=in_specs, out_specs=out_specs, check_vma=False)
```

profile of v0, /device:TPU:1, one launch (start us, length us, event | category | flops | bytes accessed | tf_op | source)
XLA Modules:
  0.0 242.7 jit_solution(9639308537524238652)
XLA Ops:
  0.7 0.8 broadcast_multiply_fusion
  1.5 0.8 copy.14
  2.3 0.1 eq.67
  2.4 0.1 eq.63
  2.6 1.5 fusion.9
  4.1 0.1 copy.13
  4.2 0.1 mul.75
  4.4 0.1 copy.16
  4.5 0.2 fusion.24
  4.8 0.2 fusion.25
  5.0 1.4 scatter_custom_fusion
  6.4 0.3 fusion.11
  6.9 4.1 %gather_fusion = bf16[384,4096]{1,0:T(8,128)(2,1)} fusion(bf16[129,4096]{1,0:T(8,128)(2,1)S(1)} %concatenate.3, s32[1024]{0:T(1024)S(1)} %pad_clamp_fusion.1), kind=kCustom, calls=%fused_computation | custom fusion | bytes 6292992 | tf_op jit(solution)/shard_map/gather | solution.py:61
  10.9 7.1 %reshape.104 = bf16[128,3,4096]{2,1,0:T(4,128)(2,1)} reshape(bf16[384,4096]{1,0:T(8,128)(2,1)} %gather_fusion) | data formatting | bytes 6291456 | tf_op jit(solution)/shard_map/reshape | solution.py:61
  18.0 64.2 %all_to_all.10 = bf16[128,3,4096]{2,1,0:T(4,128)(2,1)} all-to-all(bf16[128,3,4096]{2,1,0:T(4,128)(2,1)} %reshape.104), channel_id=1, replica_groups=mesh['expert_0'=4,'expert_1'=4,'expert_2'=4,'expert_3'=2] {'expert_0','e..., dimensions={0} | all-to-all | bytes 6291456 | tf_op jit(solution)/shard_map/all_to_all | solution.py:62
  82.2 7.4 %reshape.105 = bf16[384,4096]{1,0:T(8,128)(2,1)} reshape(bf16[128,3,4096]{2,1,0:T(4,128)(2,1)} %all_to_all.10) | data formatting | bytes 6291456 | tf_op jit(solution)/shard_map/reshape | solution.py:18
  89.6 7.4 %fusion.4 = f32[384,768]{1,0:T(8,128)} fusion(bf16[384,4096]{1,0:T(8,128)(2,1)} %reshape.105, bf16[1,4096,768]{2,1,0:T(8,128)(2,1)} %param.14), kind=kOutput, calls=%fused_computation.7 | convolution fusion | flops 2415919104 | bytes 10616832 | tf_op jit(solution)/shard_map/dot_general | solution.py:19
  97.0 14.2 %fusion.6 = bf16[384,4096]{1,0:T(8,128)(2,1)} fusion(bf16[1,768,4096]{2,1,0:T(8,128)(2,1)} %param.16, bf16[384,4096]{1,0:T(8,128)(2,1)} %reshape.105, bf16[1,4096,768]{2,1,0:T(8,128)(2,1)} %param.15, f32[384,768]{1,0:T(8,128)} %fusion.4), kind=kOutput, calls=%fused_computation.9 | convolution fusion | flops 4835180544 | bytes 20054016 | tf_op jit(solution)/shard_map/dot_general | solution.py:22
  111.2 7.1 %reshape.106 = bf16[128,3,4096]{2,1,0:T(4,128)(2,1)} reshape(bf16[384,4096]{1,0:T(8,128)(2,1)} %fusion.6) | data formatting | bytes 6291456 | tf_op jit(solution)/shard_map/reshape | solution.py:23
  118.3 6.1 %all-to-all-start.1 = ((bf16[128,3,4096]{2,1,0:T(4,128)(2,1)}), bf16[128,3,4096]{2,1,0:T(4,128)(2,1)}, u32[]{:S(2)}, u32[]{:S(2)}) async-start(bf16[128,3,4096]{2,1,0:T(4,128)(2,1)} %reshape.106), calls=%async_computation.1 | async-start | bytes 8388608 | tf_op jit(solution)/shard_map/all_to_all | solution.py:64
  124.5 0.5 select_reduce_fusion.1
  125.0 51.7 %all-to-all-done.1 = bf16[128,3,4096]{2,1,0:T(4,128)(2,1)} async-done(((bf16[128,3,4096]{2,1,0:T(4,128)(2,1)}), bf16[128,3,4096]{2,1,0:T(4,128)(2,1)}, u32[]{:S(2)}, u32[]{:S(2)}) %all-to-all-start.1) | async-done | bytes 3145760 | tf_op jit(solution)/shard_map/all_to_all | solution.py:64
  176.8 7.4 %reshape.107 = bf16[384,4096]{1,0:T(8,128)(2,1)} reshape(bf16[128,3,4096]{2,1,0:T(4,128)(2,1)} %all-to-all-done.1) | data formatting | bytes 6291456 | tf_op jit(solution)/shard_map/reshape | solution.py:65
  184.2 7.5 %gather_fusion.1 = bf16[256,4096]{1,0:T(8,128)(2,1)} fusion(bf16[384,4096]{1,0:T(8,128)(2,1)} %reshape.107, s32[1024]{0:T(1024)S(1)} %pad_clamp_fusion), kind=kCustom, calls=%fused_computation.1 | custom fusion | bytes 4195328 | tf_op jit(solution)/shard_map/gather | solution.py:66
  191.7 3.2 %reshape.108 = bf16[128,2,4096]{2,1,0:T(2,128)(2,1)S(1)} reshape(bf16[256,4096]{1,0:T(8,128)(2,1)} %gather_fusion.1) | data formatting | bytes 4194304 | tf_op jit(solution)/shard_map/reshape | solution.py:66
  194.9 4.7 %fusion.33 = (bf16[128,1,4096]{2,1,0:T(2,128)(2,1)S(1)}, bf16[128,1,4096]{2,1,0:T(2,128)(2,1)S(1)}) fusion(bf16[128,2,4096]{2,1,0:T(2,128)(2,1)S(1)} %reshape.108), kind=kLoop, calls=%fused_computation.61 | loop fusion | bytes 4194304 | tf_op jit(solution)/shard_map/slice | solution.py:69
  199.6 4.2 %fusion.13 = bf16[128,4096]{1,0:T(8,128)(2,1)S(1)} fusion(bf16[128,4096]{1,0:T(8,128)(2,1)S(1)} %copy-done.2, bf16[128,1,4096]{2,1,0:T(2,128)(2,1)S(1)} %get-tuple-element.16, bf16[128,1,4096]{2,1,0:T(2,128)(2,1)S(1)} %get-tuple-element.15, f32[128]{0:T(128)S(1)} %get-tuple-element.18, f32[128]{0:T(128)S(1)} %get-tuple-element.17), kind=kLoop, calls=%fused_computation.17 | loop fusion | flops 4194304 | bytes 4195328 | tf_op jit(solution)/shard_map/convert_element_type | solution.py:71
  203.8 1.5 fusion.32
  205.3 7.5 %all-reduce.3 = (f32[]{:T(128)}, f32[]{:T(128)}) all-reduce(f32[]{:T(128)} %get-tuple-element.6, f32[]{:T(128)} %get-tuple-element.5), channel_id=1, replica_groups=mesh['expert_0'=4,'expert_1'=4,'expert_2'=4,'expert_3'=2] {'expert_0'}, use_global_device_ids=true, to_apply=%region_8.9 | all-reduce | flops 2 | bytes 16 | tf_op jit(solution)/shard_map/psum | solution.py:12
  212.8 7.5 %all-reduce.2 = (f32[]{:T(128)}, f32[]{:T(128)}) all-reduce(f32[]{:T(128)} %get-tuple-element.11, f32[]{:T(128)} %get-tuple-element.12), channel_id=1, replica_groups=mesh['expert_0'=4,'expert_1'=4,'expert_2'=4,'expert_3'=2] {'expert_1'}, use_global_device_ids=true, to_apply=%region_9.10 | all-reduce | flops 2 | bytes 16 | tf_op jit(solution)/shard_map/psum | solution.py:12
  220.3 8.0 %all-reduce.1 = (f32[]{:T(128)}, f32[]{:T(128)}) all-reduce(f32[]{:T(128)} %get-tuple-element.9, f32[]{:T(128)} %get-tuple-element.10), channel_id=1, replica_groups=mesh['expert_0'=4,'expert_1'=4,'expert_2'=4,'expert_3'=2] {'expert_2'}, use_global_device_ids=true, to_apply=%region_10.11 | all-reduce | flops 2 | bytes 16 | tf_op jit(solution)/shard_map/psum | solution.py:12
  228.3 12.0 %all-reduce.4 = (f32[]{:T(128)}, f32[]{:T(128)}) all-reduce(f32[]{:T(128)} %get-tuple-element.7, f32[]{:T(128)} %get-tuple-element.8), channel_id=1, replica_groups=mesh['expert_0'=4,'expert_1'=4,'expert_2'=4,'expert_3'=2] {'expert_3'}, use_global_device_ids=true, to_apply=%region_11.12 | all-reduce | flops 2 | bytes 16 | tf_op jit(solution)/shard_map/psum | solution.py:12
  (35 shorter events, 0.3 us)
Async XLA Ops:
  0.6 123.8 %copy-start = (bf16[4096,128]{1,0:T(8,128)(2,1)S(1)}, bf16[4096,128]{1,0:T(8,128)(2,1)}, u32[]{:S(2)}) copy-start(bf16[4096,128]{1,0:T(8,128)(2,1)} %param.12) | copy-start | bytes 3145732
  0.6 5.8 %copy-start.1 = (bf16[128,4096]{1,0:T(8,128)(2,1)S(1)}, bf16[128,4096]{1,0:T(8,128)(2,1)}, u32[]{:S(2)}) copy-start(bf16[128,4096]{1,0:T(8,128)(2,1)} %param.10) | copy-start | bytes 3145732
  0.7 5.8 %copy-start.4 = (f32[4096]{0:T(1024)S(1)}, f32[4096]{0:T(1024)}, u32[]{:S(2)}) copy-start(f32[4096]{0:T(1024)} %param.11) | copy-start | bytes 49156
  118.3 6.1 %copy-start.6 = (bf16[4096]{0:T(1024)(128)(2,1)S(1)}, bf16[4096]{0:T(1024)(128)(2,1)}, u32[]{:S(2)}) copy-start(bf16[4096]{0:T(1024)(128)(2,1)} %param.17) | copy-start | bytes 24580
  118.3 6.2 %copy-start.5 = (s32[128,2]{0,1:T(2,128)S(1)}, s32[128,2]{0,1:T(2,128)}, u32[]{:S(2)}) copy-start(s32[128,2]{0,1:T(2,128)} %param.13) | copy-start | bytes 3076
  118.3 58.5 %all-to-all-start.1 = ((bf16[128,3,4096]{2,1,0:T(4,128)(2,1)}), bf16[128,3,4096]{2,1,0:T(4,128)(2,1)}, u32[]{:S(2)}, u32[]{:S(2)}) async-start(bf16[128,3,4096]{2,1,0:T(4,128)(2,1)} %reshape.106), calls=%async_computation.1 | async-start | bytes 8388608 | tf_op jit(solution)/shard_map/all_to_all | solution.py:64
  194.9 4.7 %copy-start.2 = (bf16[128,4096]{1,0:T(8,128)(2,1)S(1)}, bf16[128,4096]{1,0:T(8,128)(2,1)}, u32[]{:S(2)}) copy-start(bf16[128,4096]{1,0:T(8,128)(2,1)} %param.10) | copy-start | bytes 3145732
  199.6 4.2 %copy-start.7 = (f32[128]{0:T(128)S(1)}, f32[128]{0:T(128)}, u32[]{:S(2)}) copy-start(f32[128]{0:T(128)} %param.19) | copy-start | bytes 1540
  199.6 4.2 %copy-start.8 = (s32[128]{0:T(128)S(1)}, s32[128]{0:T(128)}, u32[]{:S(2)}) copy-start(s32[128]{0:T(128)} %param.18) | copy-start | bytes 1540
  203.8 37.7 %copy-start.3 = (bf16[128,4096]{1,0:T(8,128)(2,1)}, bf16[128,4096]{1,0:T(8,128)(2,1)S(1)}, u32[]{:S(2)}) copy-start(bf16[128,4096]{1,0:T(8,128)(2,1)S(1)} %fusion.13) | copy-start | bytes 3145732
where the time goes:
time: 244 us; the launch traced here: 243 us
  blocking collectives  99.1 us (41%)
  waiting for transfers between devices  51.7 us (21%)
  local copies, waits for them, and re-layouts  51.5 us (21%)
  matrix products  23.6 us (10%)
  other arithmetic  7.35 us (3%)
  starting transfers between devices  6.1 us (2%)
  between operations  3.29 us (1%)
    all_to_all x1, blocking collectives, body(): lax.all_to_all(outgoing, EXPERT, split_axis=0, concat_axis=0, tiled=True)  64.2 us
    all_to_all x1, waiting for transfers between devices, body(): lax.all_to_all(produced, EXPERT, split_axis=0, concat_axis=0, tiled=True)  51.7 us
    psum x4, blocking collectives, by_axis(): x = lax.psum(x, axis)  34.9 us
    dot_general x1, matrix products, expert_ffn(): jnp.dot(hidden, down_proj[0], preferred_element_type=jnp.float32)  14.2 us
    gather x1, local copies, waits for them, and re-layouts, body(): picked = flat_back[slot_index].reshape(token_count, 2, width)  7.53 us
    reshape x1, local copies, waits for them, and re-layouts, body(): flat_back = returned.reshape(expert_total * capacity, width)  7.42 us
    reshape x1, local copies, waits for them, and re-layouts, expert_ffn(): flat_input = received.reshape(sources * slots, width)  7.4 us
    dot_general x1, matrix products, expert_ffn(): jnp.dot(flat_input, gate_proj[0], preferred_element_type=jnp.float32)  7.38 us
  transfers between devices with their start and end apart: 1, of which 1 were waited for; matrix products, arithmetic and copies ran while one was open for 0% of the time, Pallas kernels for 0%

commit v1 on v0

v1 whole, which is shorter than its diff:
```python
import jax
import jax.numpy as jnp
from jax import lax
from jax.experimental import pallas as pl
from jax.experimental.pallas import tpu as pltpu
from jax.sharding import Mesh
from jax.sharding import PartitionSpec as P

EXPERT = ("expert_0", "expert_1", "expert_2", "expert_3")
F32 = jnp.float32
BF16 = jnp.bfloat16
I32 = jnp.int32
LANES = 128
SLOTS = 3
ROWS = 16


def vmem():
    return pl.BlockSpec(memory_space=pltpu.VMEM)


def smem():
    return pl.BlockSpec(memory_space=pltpu.SMEM)


def to_row(column):
    count = column.shape[0]
    at_row = lax.broadcasted_iota(I32, (count, count), 0)
    at_lane = lax.broadcasted_iota(I32, (count, count), 1)
    spread = jnp.where(at_row == at_lane, column, jnp.zeros_like(column))
    return jnp.sum(spread, axis=0, keepdims=True)


def route_kernel(tok_ref, gain_ref, router_ref, ids_ref, *refs):
    out_ref, gates_ref, where_ref, normed_ref, tall_ref, index_ref, index_smem, sem = refs
    count, width = tok_ref.shape
    parts = width // LANES
    experts = router_ref.shape[1]
    gain = gain_ref[...]

    def norm_rows(step, carry):
        start = pl.multiple_of(step * ROWS, ROWS)
        wide = tok_ref[pl.ds(start, ROWS), :].astype(F32)
        inverse = lax.rsqrt(jnp.mean(wide * wide, axis=1, keepdims=True) + 1e-05)
        normed = (wide * inverse * gain).astype(BF16)
        normed_ref[pl.ds(start, ROWS), :] = normed
        tall = normed.astype(F32).reshape(ROWS, parts, LANES)
        tall_ref[pl.ds(start, ROWS)] = tall.astype(BF16)
        return carry

    lax.fori_loop(0, count // ROWS, norm_rows, 0)
    tall_ref[count] = jnp.zeros((parts, LANES), BF16)

    ids = ids_ref[...]
    id_rows = [to_row(ids[:, k:k + 1]) for k in range(2)]
    expert_at = lax.broadcasted_iota(I32, (experts, count), 0)
    token_at = lax.broadcasted_iota(I32, (experts, count), 1)
    hits = [expert_at == row for row in id_rows]
    named = jnp.where(hits[0] | hits[1], 1.0, 0.0)
    before = jnp.where(
        lax.broadcasted_iota(I32, (count, count), 0) < lax.broadcasted_iota(I32, (count, count), 1), 1.0, 0.0
    )
    rank = jnp.dot(named.astype(BF16), before.astype(BF16), preferred_element_type=F32)
    rank = rank.astype(I32)
    for k in range(2):
        slot_of = jnp.sum(jnp.where(hits[k], rank, 0), axis=0, keepdims=True)
        where_ref[k:k + 1, :] = id_rows[k] * SLOTS + slot_of
    where_ref[2:, :] = jnp.zeros((where_ref.shape[0] - 2, count), I32)
    index_ref[...] = jnp.full(index_ref.shape, count, I32)
    for s in range(SLOTS):
        chosen = (hits[0] | hits[1]) & (rank == s)
        source = jnp.sum(jnp.where(chosen, token_at - count, 0), axis=1, keepdims=True) + count
        index_ref[s:s + 1, :] = to_row(source)
    copy = pltpu.make_async_copy(index_ref, index_smem, sem)
    copy.start()

    logits = jnp.dot(normed_ref[...], router_ref[...], preferred_element_type=F32)
    logits = jnp.transpose(logits)
    scores = [jnp.sum(jnp.where(hit, logits, 0.0), axis=0, keepdims=True) for hit in hits]
    gates_ref[0:1, :] = jax.nn.sigmoid(scores[0] - scores[1])
    gates_ref[1:2, :] = jax.nn.sigmoid(scores[1] - scores[0])
    gates_ref[2:, :] = jnp.zeros((gates_ref.shape[0] - 2, count), F32)
    copy.wait()

    for s in range(SLOTS):
        def send(step, carry, s=s):
            for i in range(8):
                e = step * 8 + i
                out_ref[e, s * parts:(s + 1) * parts] = tall_ref[index_smem[s, e]]
            return carry

        lax.fori_loop(0, experts // 8, send, 0)


def route(tokens, norm_gain, router_weight, expert_ids):
    count, width = tokens.shape
    experts = router_weight.shape[1]
    parts = width // LANES
    return pl.pallas_call(
        route_kernel,
        in_specs=[vmem()] * 4,
        out_specs=[vmem()] * 3,
        out_shape=[
            jax.ShapeDtypeStruct((experts, SLOTS * parts, LANES), BF16),
            jax.ShapeDtypeStruct((8, count), F32),
            jax.ShapeDtypeStruct((8, count), I32),
        ],
        scratch_shapes=[
            pltpu.VMEM((count, width), BF16),
            pltpu.VMEM((count + 1, parts, LANES), BF16),
            pltpu.VMEM((8, experts), I32),
            pltpu.SMEM((8, experts), I32),
            pltpu.SemaphoreType.DMA(()),
        ],
        name="route",
    )(tokens, norm_gain.reshape(1, width), router_weight, expert_ids)


def ffn_kernel(in_ref, gate_ref, up_ref, down_ref, out_ref, wide_ref, sum_ref):
    sources = in_ref.shape[0]
    width = wide_ref.shape[1]
    parts = width // LANES
    step = pl.program_id(0)

    @pl.when(step == 0)
    def _():
        for s in range(SLOTS):
            def widen(i, carry, s=s):
                start = pl.multiple_of(i * ROWS, ROWS)
                tall = in_ref[pl.ds(start, ROWS), s * parts:(s + 1) * parts].astype(F32)
                wide_ref[pl.ds(s * sources + start, ROWS), :] = tall.reshape(ROWS, width).astype(BF16)
                return carry

            lax.fori_loop(0, sources // ROWS, widen, 0)

    x = wide_ref[...]
    gate = jnp.dot(x, gate_ref[0], preferred_element_type=F32)
    up = jnp.dot(x, up_ref[0], preferred_element_type=F32)
    hidden = (jax.nn.silu(gate) * up).astype(BF16)
    part = jnp.dot(hidden, down_ref[0], preferred_element_type=F32)

    @pl.when(step == 0)
    def _():
        sum_ref[...] = part

    @pl.when(step > 0)
    def _():
        sum_ref[...] += part

    @pl.when(step == pl.num_programs(0) - 1)
    def _():
        for s in range(SLOTS):
            def heighten(i, carry, s=s):
                start = pl.multiple_of(i * ROWS, ROWS)
                wide = sum_ref[pl.ds(s * sources + start, ROWS), :]
                tall = wide.reshape(ROWS, parts, LANES).astype(BF16)
                out_ref[pl.ds(start, ROWS), s * parts:(s + 1) * parts] = tall
                return carry

            lax.fori_loop(0, sources // ROWS, heighten, 0)


def expert_ffn(received, gate_proj, up_proj, down_proj):
    sources = received.shape[0]
    _, width, hidden = gate_proj.shape
    tile = 256
    rows = SLOTS * sources
    return pl.pallas_call(
        ffn_kernel,
        grid=(hidden // tile,),
        in_specs=[
            vmem(),
            pl.BlockSpec((1, width, tile), lambda i: (0, 0, i)),
            pl.BlockSpec((1, width, tile), lambda i: (0, 0, i)),
            pl.BlockSpec((1, tile, width), lambda i: (0, i, 0)),
        ],
        out_specs=vmem(),
        out_shape=jax.ShapeDtypeStruct(received.shape, BF16),
        scratch_shapes=[pltpu.VMEM((rows, width), BF16), pltpu.VMEM((rows, width), F32)],
        compiler_params=pltpu.CompilerParams(vmem_limit_bytes=56 * 1024 * 1024),
        name="ffn",
    )(received, gate_proj, up_proj, down_proj)


def mix_kernel(
    tok_ref, back_ref, gates_ref, where_ref, weight_ref, target_ref, recency_ref,
    mixed_ref, values_ref, parts_ref, sum_ref,
):
    count, width = tok_ref.shape
    parts = width // LANES
    weight = weight_ref[...].astype(F32)

    def mix_rows(step, carry):
        start = pl.multiple_of(step * ROWS, ROWS)
        for i in range(ROWS):
            t = start + i
            total = None
            for k in range(2):
                at = where_ref[k, t]
                row = back_ref[at].astype(F32) * gates_ref[k, t]
                total = row if total is None else total + row
            sum_ref[i] = total
        update = sum_ref[...].reshape(ROWS, width)
        mixed = (tok_ref[pl.ds(start, ROWS), :].astype(F32) + update).astype(BF16)
        mixed_ref[pl.ds(start, ROWS), :] = mixed
        return carry

    lax.fori_loop(0, count // ROWS, mix_rows, 0)

    products = mixed_ref[...].astype(F32) * weight
    values = jnp.tanh(to_row(jnp.sum(products, axis=1, keepdims=True)))
    values_ref[...] = values
    error = values - target_ref[...].astype(F32)
    recency = recency_ref[...]
    weighted = jnp.sum(recency * error * error, axis=1, keepdims=True)
    total = jnp.sum(recency, axis=1, keepdims=True)
    lane = lax.broadcasted_iota(I32, parts_ref.shape, 1)
    parts_ref[...] = jnp.where(lane == 0, weighted, jnp.where(lane == 1, total, 0.0))


def mix(tokens, back, gates, where, value_weight, value_target, recency, devices):
    count, width = tokens.shape
    parts = width // LANES
    return pl.pallas_call(
        mix_kernel,
        in_specs=[vmem()] * 2 + [smem()] * 2 + [vmem()] * 3,
        out_specs=[vmem()] * 3,
        out_shape=[
            jax.ShapeDtypeStruct((count, width), BF16),
            jax.ShapeDtypeStruct((1, count), F32),
            jax.ShapeDtypeStruct((devices, LANES), F32),
        ],
        scratch_shapes=[pltpu.VMEM((ROWS, parts, LANES), F32)],
        name="mix",
    )(
        tokens, back.reshape(devices * SLOTS, parts, LANES), gates, where, value_weight.reshape(1, width),
        value_target.reshape(1, count), recency.reshape(1, count),
    )


def exchange(x):
    return lax.all_to_all(x, EXPERT, split_axis=0, concat_axis=0, tiled=True)


def body(
    tokens,
    norm_gain,
    router_weight,
    expert_ids,
    gate_proj,
    up_proj,
    down_proj,
    value_weight,
    value_target,
    recency,
):
    count, width = tokens.shape
    experts = router_weight.shape[1]
    outgoing, gates, where = route(tokens, norm_gain, router_weight, expert_ids)
    produced = expert_ffn(exchange(outgoing), gate_proj, up_proj, down_proj)
    back = exchange(produced)
    mixed, values, sums = mix(
        tokens, back, gates, where, value_weight, value_target, recency, experts
    )
    everyone = exchange(sums.reshape(experts, 1, LANES)).reshape(experts, LANES)
    total = jnp.sum(everyone, axis=0)
    return (mixed, values.reshape(count), total[0] / total[1])


def solution(mesh):
    finer = Mesh(mesh.devices.reshape(4, 4, 4, 2), EXPERT)
    in_specs = (
        P(EXPERT, None),
        P(),
        P(),
        P(EXPERT, None),
        P(EXPERT, None, None),
        P(EXPERT, None, None),
        P(EXPERT, None, None),
        P(),
        P(EXPERT),
        P(EXPERT),
    )
    out_specs = (P(EXPERT, None), P(EXPERT), P())
    return jax.shard_map(body, mesh=finer, in_specs=in_specs, out_specs=out_specs, check_vma=False)
```

time: 244 us -> 151 us (0.62)
  local copies, waits for them, and re-layouts: 51.5 us -> 4.25 us
  blocking collectives: 99.1 us -> 67.5 us
  Pallas kernels: 0 us -> 29.5 us
  matrix products: 23.6 us -> 0 us
  waiting for transfers between devices: 51.7 us -> 40.7 us
  other arithmetic: 7.35 us -> 0.15 us
    psum x4 -> x0, blocking collectives: 34.9 us -> none  [by_axis(): x = lax.psum(x, axis)]
    reshape x5 -> x1, local copies, waits for them, and re-layouts: 32.2 us -> 0.61 us  [mix(): value_weight.reshape(1, width)]
    pallas_call x0 -> x3, Pallas kernels: none -> 29.5 us  [the longest x1 18.3 us: expert_ffn(): pl.pallas_call(ffn_kernel, grid=(hidden // tile,), in_specs=[vmem(), pl.B...]
    dot_general x4 -> x0, matrix products: 23.6 us -> none  [the longest x1 14.2 us: expert_ffn(): jnp.dot(hidden, down_proj[0], preferred_element_type=jnp.float32)]
    gather x2 -> x0, local copies, waits for them, and re-layouts: 11.6 us -> none  [the longest x1 7.53 us: body(): picked = flat_back[slot_index].reshape(token_count, 2, width)]
    all_to_all x1, waiting for transfers between devices: 51.7 us -> 40.7 us  [exchange(): return lax.all_to_all(x, EXPERT, split_axis=0, concat_axis=0, tiled=True)]
    convert_element_type x2 -> x0, other arithmetic: 4.51 us -> none  [the longest x1 4.19 us: body(): mixed = (wide + gate_first[:, None] * picked[:, 0].astype(jnp.float32) +...]
    slice x1, local copies, waits for them, and re-layouts: 4.69 us -> 0.59 us  [body(): return (mixed, values.reshape(count), total[0] / total[1])]
where the time goes in v1:
time: 151 us; the launch traced here: 150 us
  blocking collectives  67.5 us (45%)
  waiting for transfers between devices  40.7 us (27%)
  Pallas kernels  29.5 us (20%)
  starting transfers between devices  5.16 us (3%)
  local copies, waits for them, and re-layouts  4.25 us (3%)
  between operations  3.1 us (2%)
    all_to_all x2, blocking collectives, exchange(): return lax.all_to_all(x, EXPERT, split_axis=0, concat_axis=0, tiled=True)  67.5 us
    all_to_all x1, waiting for transfers between devices, exchange(): return lax.all_to_all(x, EXPERT, split_axis=0, concat_axis=0, tiled=True)  40.7 us
    pallas_call x1, Pallas kernels, expert_ffn(): pl.pallas_call(ffn_kernel, grid=(hidden // tile,), in_specs=[vmem(), pl.B...  18.3 us
    pallas_call x1, Pallas kernels, route(): pl.pallas_call(route_kernel, in_specs=[vmem()] * 4, out_specs=[vmem()] *...  7.06 us
    all_to_all x1, starting transfers between devices, exchange(): return lax.all_to_all(x, EXPERT, split_axis=0, concat_axis=0, tiled=True)  5.16 us
    pallas_call x1, Pallas kernels, mix(): pl.pallas_call(mix_kernel, in_specs=[vmem()] * 2 + [smem()] * 2 + [vmem()...  4.22 us
    unnamed x5, local copies, waits for them, and re-layouts  3.06 us
  transfers between devices with their start and end apart: 1, of which 1 were waited for; matrix products, arithmetic and copies ran while one was open for 0% of the time, Pallas kernels for 0%

profile of v1, /device:TPU:1, one launch (start us, length us, event | category | flops | bytes accessed | tf_op | source)
XLA Modules:
  0.0 150.4 jit_solution(7655173581395379580)
XLA Ops:
  0.6 1.4 copy.14.ids_ref
  2.0 7.1 %route.1 = (bf16[128,96,128]{2,1,0:T(8,128)(2,1)}, f32[8,128]{1,0:T(8,128)}, s32[8,128]{1,0:T(8,128)}) custom-call(bf16[128,4096]{1,0:T(8,128)(2,1)} %tok_ref.3, f32[1,4096]{1,0:T(1,128)} %bitcast.11, bf16[4096,128]{1,0:T(8,128)(2,1)} %router_ref.1, s32[128,2]{1,0:T(8,128)} %copy.14.ids_ref), custom_call_target="tpu_custom_call" | custom-call | tf_op jit(solution)/shard_map/route/pallas_call | solution.py:99
  9.1 52.8 %all_to_all.15.in_ref = bf16[128,96,128]{2,1,0:T(8,128)(2,1)} all-to-all(bf16[128,96,128]{2,1,0:T(8,128)(2,1)} %get-tuple-element.9), channel_id=1, replica_groups=mesh['expert_0'=4,'expert_1'=4,'expert_2'=4,'expert_3'=2] {'expert_0','e..., dimensions={0} | all-to-all | bytes 6291456 | tf_op jit(solution)/shard_map/all_to_all | solution.py:242
  61.9 18.3 %ffn.1 = bf16[128,96,128]{2,1,0:T(8,128)(2,1)} custom-call(bf16[128,96,128]{2,1,0:T(8,128)(2,1)} %all_to_all.15.in_ref, bf16[1,4096,768]{2,1,0:T(8,128)(2,1)} %gate_ref.1, bf16[1,4096,768]{2,1,0:T(8,128)(2,1)} %up_ref.1, bf16[1,768,4096]{2,1,0:T(8,128)(2,1)} %down_ref.1), custom_call_target="tpu_custom_call" | custom-call | tf_op jit(solution)/shard_map/ffn/pallas_call | solution.py:168
  80.1 0.0 copy-start.1
  80.1 5.2 %all-to-all-start.1 = ((bf16[128,96,128]{2,1,0:T(8,128)(2,1)}), bf16[128,96,128]{2,1,0:T(8,128)(2,1)S(1)}, u32[]{:S(2)}, u32[]{:S(2)}) async-start(bf16[128,96,128]{2,1,0:T(8,128)(2,1)} %ffn.1), calls=%async_computation.1 | async-start | bytes 6291456 | tf_op jit(solution)/shard_map/all_to_all | solution.py:242
  85.3 0.0 copy-done.1
  85.3 0.6 reshape.31.weight_ref
  85.9 40.7 %all-to-all-done.1 = bf16[128,96,128]{2,1,0:T(8,128)(2,1)S(1)} async-done(((bf16[128,96,128]{2,1,0:T(8,128)(2,1)}), bf16[128,96,128]{2,1,0:T(8,128)(2,1)S(1)}, u32[]{:S(2)}, u32[]{:S(2)}) %all-to-all-start.1) | async-done | bytes 3145760 | tf_op jit(solution)/shard_map/all_to_all | solution.py:242
  126.6 0.0 copy-start
  126.6 1.6 %copy-done = bf16[128,96,128]{2,1,0:T(8,128)(2,1)} copy-done((bf16[128,96,128]{2,1,0:T(8,128)(2,1)}, bf16[128,96,128]{2,1,0:T(8,128)(2,1)S(1)}, u32[]{:S(2)}) %copy-start) | copy-done | bytes 3145752
  128.3 4.2 %mix.1 = (bf16[128,4096]{1,0:T(8,128)(2,1)}, f32[1,128]{1,0:T(1,128)}, f32[128,128]{1,0:T(8,128)}) custom-call(bf16[128,4096]{1,0:T(8,128)(2,1)} %tok_ref.3, bf16[384,32,128]{2,1,0:T(8,128)(2,1)} %bitcast.9, f32[8,128]{1,0:T(8,128)} %get-tuple-element.10.gates_ref, s32[8,128]{1,0:T(8,128)} %get-tuple-element.11.where_ref, ...), custom_call_target="tpu_custom_call" | custom-call | tf_op jit(solution)/shard_map/mix/pallas_call | solution.py:224
  132.5 14.8 %all_to_all.16 = f32[128,1,128]{2,1,0:T(1,128)S(1)} all-to-all(f32[128,1,128]{2,1,0:T(1,128)} %bitcast.10), channel_id=1, replica_groups=mesh['expert_0'=4,'expert_1'=4,'expert_2'=4,'expert_3'=2] {'expert_0','e..., dimensions={0} | all-to-all | bytes 131072 | tf_op jit(solution)/shard_map/all_to_all | solution.py:242
  147.2 0.2 reduce_sum.9
  147.4 0.6 fusion
Async XLA Ops:
  80.1 5.2 %copy-start.1 = (bf16[4096]{0:T(1024)(128)(2,1)S(1)}, bf16[4096]{0:T(1024)(128)(2,1)}, u32[]{:S(2)}) copy-start(bf16[4096]{0:T(1024)(128)(2,1)} %param.17) | copy-start | bytes 24580
  80.1 46.5 %all-to-all-start.1 = ((bf16[128,96,128]{2,1,0:T(8,128)(2,1)}), bf16[128,96,128]{2,1,0:T(8,128)(2,1)S(1)}, u32[]{:S(2)}, u32[]{:S(2)}) async-start(bf16[128,96,128]{2,1,0:T(8,128)(2,1)} %ffn.1), calls=%async_computation.1 | async-start | bytes 6291456 | tf_op jit(solution)/shard_map/all_to_all | solution.py:242
  126.6 1.6 %copy-start = (bf16[128,96,128]{2,1,0:T(8,128)(2,1)}, bf16[128,96,128]{2,1,0:T(8,128)(2,1)S(1)}, u32[]{:S(2)}) copy-start(bf16[128,96,128]{2,1,0:T(8,128)(2,1)S(1)} %all-to-all-done.1) | copy-start | bytes 9437188

commit v2 on v0

v2 whole, which is shorter than its diff:
```python
import jax
import jax.numpy as jnp
from jax import lax
from jax.experimental import pallas as pl
from jax.experimental.pallas import tpu as pltpu
from jax.sharding import Mesh
from jax.sharding import PartitionSpec as P

EXPERT = ("expert_0", "expert_1", "expert_2", "expert_3")
F32 = jnp.float32
BF16 = jnp.bfloat16
I32 = jnp.int32
LANES = 128
SLOTS = 3
ROWS = 16
CHUNKS = 4
MIB = 1024 * 1024
NEAR = pl.BlockSpec(memory_space=pltpu.VMEM)
SCALARS = pl.BlockSpec(memory_space=pltpu.SMEM)
FAR = pl.BlockSpec(memory_space=pltpu.HBM)


def params(mib):
    return pltpu.CompilerParams(vmem_limit_bytes=mib * MIB)


def cost(flops, moved):
    return pl.CostEstimate(flops=flops, transcendentals=0, bytes_accessed=moved)


def kept(x):
    return pltpu.with_memory_space_constraint(x, pltpu.VMEM)


def far(x):
    return pltpu.with_memory_space_constraint(x, pltpu.HBM)


def start_all(pairs, sems):
    copies = [pltpu.make_async_copy(src, dst, sems.at[i]) for i, (src, dst) in enumerate(pairs)]
    for copy in copies:
        copy.start()
    return copies


def pieces_of(count, pieces):
    size = count // pieces
    return [pl.ds(i * size, size) for i in range(pieces)]


def iota(shape, dim):
    return lax.broadcasted_iota(I32, shape, dim)


def to_row(column):
    count = column.shape[0]
    spread = jnp.where(iota((count, count), 0) == iota((count, count), 1), column, jnp.zeros_like(column))
    return jnp.sum(spread, axis=0, keepdims=True)


def slots_of(ids_ref, experts):
    count = ids_ref.shape[1]
    hits = [iota((experts, count), 0) == ids_ref[k:k + 1, :] for k in range(2)]
    named = jnp.where(hits[0] | hits[1], 1.0, 0.0).astype(BF16)
    before = jnp.where(iota((count, count), 0) < iota((count, count), 1), 1.0, 0.0).astype(BF16)
    rank = jnp.dot(named, before, preferred_element_type=F32)
    return hits, rank


def norm(wide, gain):
    inverse = lax.rsqrt(jnp.mean(wide * wide, axis=1, keepdims=True) + 1e-05)
    return (wide * inverse * gain).astype(BF16)


def route_kernel(
    tok_ref, gain_ref, ids_ref, out_ref,
    near_ref, gain_near, ids_near, tall_ref, piece_ref, index_ref, index_smem, sems, out_sems, index_sem,
):
    count, width = tok_ref.shape
    parts = width // LANES
    experts = out_ref.shape[0]
    copies = start_all(
        [(ids_ref, ids_near), (gain_ref, gain_near)]
        + [(tok_ref.at[rows], near_ref.at[rows]) for rows in pieces_of(count, CHUNKS)],
        sems,
    )
    copies[0].wait()
    hits, rank = slots_of(ids_near, experts)
    named = hits[0] | hits[1]
    token = (iota((8, count), 1) - count).astype(F32).astype(BF16)
    for s in range(SLOTS):
        chosen = jnp.where(named & (rank == s), 1.0, 0.0).astype(BF16)
        source = lax.dot_general(token, chosen, (((1,), (1,)), ((), ())), preferred_element_type=F32)
        index_ref[s:s + 1, :] = source[0:1].astype(I32) + count
    index_ref[SLOTS:, :] = jnp.zeros((8 - SLOTS, experts), I32)
    index_copy = pltpu.make_async_copy(index_ref, index_smem, index_sem)
    index_copy.start()
    tall_ref[count] = jnp.zeros((parts, LANES), BF16)
    copies[1].wait()
    gain = gain_near[...]
    chunk = count // CHUNKS
    for c in range(CHUNKS):
        copies[2 + c].wait()

        def norm_rows(step, carry, c=c):
            start = pl.multiple_of(c * chunk + step * ROWS, ROWS)
            normed = norm(near_ref[pl.ds(start, ROWS), :].astype(F32), gain)
            tall_ref[pl.ds(start, ROWS)] = normed.astype(F32).reshape(ROWS, parts, LANES).astype(BF16)
            return carry

        lax.fori_loop(0, chunk // ROWS, norm_rows, 0)
    index_copy.wait()
    chunk = experts // CHUNKS
    sent = []
    for c, rows in enumerate(pieces_of(experts, CHUNKS)):
        def send(step, carry, c=c):
            for i in range(4):
                e = c * chunk + step * 4 + i
                for s in range(SLOTS):
                    piece_ref[e, s * parts:(s + 1) * parts] = tall_ref[index_smem[s, e]]
            return carry

        lax.fori_loop(0, chunk // 4, send, 0)
        sent.append(pltpu.make_async_copy(piece_ref.at[rows], out_ref.at[rows], out_sems.at[c]))
        sent[c].start()
    for copy in sent:
        copy.wait()


def route(tokens, norm_gain, ids, experts):
    count, width = tokens.shape
    parts = width // LANES
    pieces = (experts, SLOTS * parts, LANES)
    return pl.pallas_call(
        route_kernel,
        in_specs=[FAR] * 3,
        out_specs=FAR,
        out_shape=pltpu.HBM(pieces, BF16),
        scratch_shapes=[
            pltpu.VMEM((count, width), BF16),
            pltpu.VMEM(norm_gain.shape, F32),
            pltpu.VMEM(ids.shape, I32),
            pltpu.VMEM((count + 1, parts, LANES), BF16),
            pltpu.VMEM(pieces, BF16),
            pltpu.VMEM((8, experts), I32),
            pltpu.SMEM((8, experts), I32),
            pltpu.SemaphoreType.DMA((2 + CHUNKS,)),
            pltpu.SemaphoreType.DMA((CHUNKS,)),
            pltpu.SemaphoreType.DMA(()),
        ],
        compiler_params=params(16),
        name="route",
    )(far(tokens), far(norm_gain), far(ids))


def gate_kernel(tok_ref, gain_ref, router_ref, ids_ref, gates_ref, where_ref, tall_ref, normed_ref):
    count, width = tok_ref.shape
    parts = width // LANES
    experts = router_ref.shape[1]
    gain = gain_ref[...]

    def norm_rows(step, carry):
        start = pl.multiple_of(step * ROWS, ROWS)
        wide = tok_ref[pl.ds(start, ROWS), :].astype(F32)
        normed_ref[pl.ds(start, ROWS), :] = norm(wide, gain)
        tall_ref[pl.ds(start, ROWS)] = wide.reshape(ROWS, parts, LANES).astype(BF16)
        return carry

    lax.fori_loop(0, count // ROWS, norm_rows, 0)
    hits, rank = slots_of(ids_ref, experts)
    logits = jnp.transpose(jnp.dot(normed_ref[...], router_ref[...], preferred_element_type=F32))
    scores = []
    where_ref[...] = jnp.zeros(where_ref.shape, I32)
    gates_ref[...] = jnp.zeros(gates_ref.shape, F32)
    for k in range(2):
        slot = jnp.sum(jnp.where(hits[k], rank, 0.0), axis=0, keepdims=True).astype(I32)
        where_ref[k:k + 1, :] = ids_ref[k:k + 1, :] * SLOTS + slot
        scores.append(jnp.sum(jnp.where(hits[k], logits, 0.0), axis=0, keepdims=True))
    gates_ref[0:1, :] = jax.nn.sigmoid(scores[0] - scores[1])
    gates_ref[1:2, :] = jax.nn.sigmoid(scores[1] - scores[0])


def gate(tokens, norm_gain, router_weight, ids):
    count, width = tokens.shape
    parts = width // LANES
    return pl.pallas_call(
        gate_kernel,
        in_specs=[NEAR] * 4,
        out_specs=[NEAR] * 3,
        out_shape=[
            jax.ShapeDtypeStruct((8, count), F32),
            jax.ShapeDtypeStruct((8, count), I32),
            pltpu.HBM((count, parts, LANES), BF16),
        ],
        scratch_shapes=[pltpu.VMEM((count, width), BF16)],
        compiler_params=params(16),
        cost_estimate=cost(10**10, 4 * MIB),
        name="gate",
    )(tokens, norm_gain, router_weight, ids)


def ffn_kernel(
    in_ref, gate_ref, up_ref, down_ref, out_ref,
    gate_near, up_near, down_near, wide_ref, hidden_ref, tall_ref, sems, out_sems,
):
    rows, parts, _ = in_ref.shape
    width, hidden = gate_near.shape
    tiles = [slice(start, start + 256) for start in range(0, hidden, 256)]
    pairs = []
    for tile in tiles:
        pairs.append((gate_ref.at[0, :, tile], gate_near.at[:, tile]))
        pairs.append((up_ref.at[0, :, tile], up_near.at[:, tile]))
    for tile in tiles:
        pairs.append((down_ref.at[0, tile, :], down_near.at[tile, :]))
    copies = start_all(pairs, sems)

    def widen(i, carry):
        start = pl.multiple_of(i * ROWS, ROWS)
        tall = in_ref[pl.ds(start, ROWS)].astype(F32)
        wide_ref[pl.ds(start, ROWS), :] = tall.reshape(ROWS, width).astype(BF16)
        return carry

    lax.fori_loop(0, rows // ROWS, widen, 0)
    for i, tile in enumerate(tiles):
        copies[2 * i].wait()
        copies[2 * i + 1].wait()
        x = wide_ref[...]
        gated = jnp.dot(x, gate_near[:, tile], preferred_element_type=F32)
        upped = jnp.dot(x, up_near[:, tile], preferred_element_type=F32)
        hidden_ref[:, tile] = (jax.nn.silu(gated) * upped).astype(BF16)
    for i in range(len(tiles)):
        copies[2 * len(tiles) + i].wait()
    for start in range(0, width, 512):
        tile = slice(start, start + 512)
        wide_ref[:, tile] = jnp.dot(hidden_ref[...], down_near[:, tile], preferred_element_type=F32).astype(BF16)
    pieces = out_sems.shape[0]
    sent = []
    for p, piece in enumerate(pieces_of(rows, pieces)):
        def heighten(i, carry, p=p):
            start = pl.multiple_of(p * (rows // pieces) + i * ROWS, ROWS)
            wide = wide_ref[pl.ds(start, ROWS), :].astype(F32)
            tall_ref[pl.ds(start, ROWS)] = wide.reshape(ROWS, parts, LANES).astype(BF16)
            return carry

        lax.fori_loop(0, rows // pieces // ROWS, heighten, 0)
        sent.append(pltpu.make_async_copy(tall_ref.at[piece], out_ref.at[piece], out_sems.at[p]))
        sent[p].start()
    for copy in sent:
        copy.wait()


def expert_ffn(received, gate_proj, up_proj, down_proj):
    rows, parts, _ = received.shape
    _, width, hidden = gate_proj.shape
    return pl.pallas_call(
        ffn_kernel,
        in_specs=[NEAR] + [FAR] * 3,
        out_specs=FAR,
        out_shape=pltpu.HBM(received.shape, BF16),
        scratch_shapes=[
            pltpu.VMEM((width, hidden), BF16),
            pltpu.VMEM((width, hidden), BF16),
            pltpu.VMEM((hidden, width), BF16),
            pltpu.VMEM((rows, width), BF16),
            pltpu.VMEM((rows, hidden), BF16),
            pltpu.VMEM((rows, parts, LANES), BF16),
            pltpu.SemaphoreType.DMA((3 * (hidden // 256),)),
            pltpu.SemaphoreType.DMA((6,)),
        ],
        compiler_params=params(40),
        cost_estimate=cost(6 * rows * width * hidden, 24 * MIB),
        name="ffn",
    )(kept(received), far(gate_proj), far(up_proj), far(down_proj))


def mix_kernel(
    back_ref, token_ref, gates_ref, where_ref, weight_ref, target_ref, recency_ref,
    mixed_ref, values_ref, sums_ref,
    tall_ref, near_ref, score_ref, sems, out_sems,
):
    count, parts, _ = token_ref.shape
    rows = pieces_of(count, CHUNKS)
    copies = start_all([(token_ref.at[r], tall_ref.at[r]) for r in rows], sems)
    weight = weight_ref[...]
    chunk = count // CHUNKS
    sent = []
    for c in range(CHUNKS):
        copies[c].wait()

        def mix_rows(step, carry, c=c):
            for i in range(8):
                t = c * chunk + step * 8 + i
                total = tall_ref[t].astype(F32)
                for k in range(2):
                    total = total + gates_ref[k, t] * back_ref[where_ref[k, t]].astype(F32)
                mixed = total.astype(BF16)
                near_ref[t] = mixed
                scored = mixed.astype(F32) * weight
                score_ref[t] = jnp.sum(scored.reshape(parts // 8, 8, LANES), axis=0)
            return carry

        lax.fori_loop(0, chunk // 8, mix_rows, 0)
        sent.append(pltpu.make_async_copy(near_ref.at[rows[c]], mixed_ref.at[rows[c]], out_sems.at[c]))
        sent[c].start()
    by_lane = jnp.sum(score_ref[...], axis=1)
    values = jnp.tanh(to_row(jnp.sum(by_lane, axis=1, keepdims=True)))
    values_ref[...] = values
    error = values - target_ref[...].astype(F32)
    recency = recency_ref[...]
    weighted = jnp.sum(recency * error * error, axis=1, keepdims=True)
    total = jnp.sum(recency, axis=1, keepdims=True)
    lane = iota(sums_ref.shape, 1)
    sums_ref[...] = jnp.where(lane == 0, weighted, jnp.where(lane == 1, total, 0.0))
    for copy in sent:
        copy.wait()


def mix(back, tall, gates, where, weight, target, recency, devices):
    count, parts, _ = tall.shape
    return pl.pallas_call(
        mix_kernel,
        in_specs=[NEAR, FAR] + [SCALARS] * 2 + [NEAR] * 3,
        out_specs=[FAR] + [NEAR] * 2,
        out_shape=[
            pltpu.HBM(tall.shape, BF16),
            jax.ShapeDtypeStruct((1, count), F32),
            jax.ShapeDtypeStruct((devices, LANES), F32),
        ],
        scratch_shapes=[
            pltpu.VMEM((count, parts, LANES), BF16),
            pltpu.VMEM((count, parts, LANES), BF16),
            pltpu.VMEM((count, 8, LANES), F32),
            pltpu.SemaphoreType.DMA((CHUNKS,)),
            pltpu.SemaphoreType.DMA((CHUNKS,)),
        ],
        compiler_params=params(16),
        name="mix",
    )(kept(back), far(tall), gates, where, weight, target, recency)


def widen_kernel(tall_ref, out_ref):
    count, width = out_ref.shape

    def widen(i, carry):
        start = pl.multiple_of(i * ROWS, ROWS)
        tall = tall_ref[pl.ds(start, ROWS)].astype(F32)
        out_ref[pl.ds(start, ROWS), :] = tall.reshape(ROWS, width).astype(BF16)
        return carry

    lax.fori_loop(0, count // ROWS, widen, 0)


def widen_rows(tall):
    count, parts, _ = tall.shape
    return pl.pallas_call(
        widen_kernel,
        in_specs=[NEAR],
        out_specs=NEAR,
        out_shape=jax.ShapeDtypeStruct((count, parts * LANES), BF16),
        compiler_params=params(8),
        cost_estimate=cost(10**10, 2 * MIB),
        name="widen",
    )(far(tall))


def exchange(x):
    return lax.all_to_all(x, EXPERT, split_axis=0, concat_axis=0, tiled=True)


def body(
    tokens,
    norm_gain,
    router_weight,
    expert_ids,
    gate_proj,
    up_proj,
    down_proj,
    value_weight,
    value_target,
    recency,
):
    count, width = tokens.shape
    experts = router_weight.shape[1]
    parts = width // LANES
    pieces = (experts, SLOTS * parts, LANES)
    rows = (experts * SLOTS, parts, LANES)
    ids = expert_ids.T
    gain = norm_gain.reshape(1, width)
    received = exchange(route(tokens, gain, ids, experts))
    gates, where, tall = gate(tokens, gain, router_weight, ids)
    produced = expert_ffn(received.reshape(rows), gate_proj, up_proj, down_proj)
    back = exchange(produced.reshape(pieces))
    mixed, values, sums = mix(
        back.reshape(rows), tall, gates, where, value_weight.reshape(parts, LANES).astype(F32),
        value_target.reshape(1, count), recency.reshape(1, count), experts,
    )
    everyone = exchange(sums.reshape(experts, 1, LANES)).reshape(experts, LANES)
    total = jnp.sum(everyone, axis=0)
    return (widen_rows(mixed), values.reshape(count), total[0] / total[1])


def solution(mesh):
    finer = Mesh(mesh.devices.reshape(4, 4, 4, 2), EXPERT)
    in_specs = (
        P(EXPERT, None),
        P(),
        P(),
        P(EXPERT, None),
        P(EXPERT, None, None),
        P(EXPERT, None, None),
        P(EXPERT, None, None),
        P(),
        P(EXPERT),
        P(EXPERT),
    )
    out_specs = (P(EXPERT, None), P(EXPERT), P())
    return jax.shard_map(body, mesh=finer, in_specs=in_specs, out_specs=out_specs, check_vma=False)
```

time: 244 us -> 139 us (0.57)
  local copies, waits for them, and re-layouts: 51.5 us -> 3.06 us
  blocking collectives: 99.1 us -> 52.7 us
  Pallas kernels: 0 us -> 25.9 us
  matrix products: 23.6 us -> 0 us
  waiting for transfers between devices: 51.7 us -> 43.6 us
  other arithmetic: 7.35 us -> 0.16 us
  starting transfers between devices: 6.1 us -> 9.96 us
    psum x4 -> x0, blocking collectives: 34.9 us -> none  [by_axis(): x = lax.psum(x, axis)]
    reshape x5 -> x0, local copies, waits for them, and re-layouts: 32.2 us -> none  [the longest x1 7.42 us: body(): flat_back = returned.reshape(expert_total * capacity, width)]
    pallas_call x0 -> x5, Pallas kernels: none -> 25.9 us  [the longest x1 12.6 us: expert_ffn(): pl.pallas_call(ffn_kernel, in_specs=[NEAR] + [FAR] * 3, out_specs=FAR, ou...]
    dot_general x4 -> x0, matrix products: 23.6 us -> none  [the longest x1 14.2 us: expert_ffn(): jnp.dot(hidden, down_proj[0], preferred_element_type=jnp.float32)]
    gather x2 -> x0, local copies, waits for them, and re-layouts: 11.6 us -> none  [the longest x1 7.53 us: body(): picked = flat_back[slot_index].reshape(token_count, 2, width)]
    all_to_all x1, blocking collectives: 64.2 us -> 52.7 us  [exchange(): return lax.all_to_all(x, EXPERT, split_axis=0, concat_axis=0, tiled=True)]
    all_to_all x1 -> x2, waiting for transfers between devices: 51.7 us -> 43.6 us  [exchange(): return lax.all_to_all(x, EXPERT, split_axis=0, concat_axis=0, tiled=True)]
    convert_element_type x2 -> x1, other arithmetic: 4.51 us -> 0.01 us  [body(): value_weight.reshape(parts, LANES).astype(F32)]
  transfers between devices with their start and end apart: 1 -> 2, of which waited for: 1 -> 2; matrix products, arithmetic and copies ran while one was open for 0% -> 0% of each run, Pallas kernels for 0% -> 3%
where the time goes in v2:
time: 139 us; the launch traced here: 138 us
  blocking collectives  52.7 us (38%)
  waiting for transfers between devices  43.6 us (31%)
  Pallas kernels  25.9 us (19%)
  starting transfers between devices  9.96 us (7%)
  between operations  3.18 us (2%)
  local copies, waits for them, and re-layouts  3.06 us (2%)
    all_to_all x1, blocking collectives, exchange(): return lax.all_to_all(x, EXPERT, split_axis=0, concat_axis=0, tiled=True)  52.7 us
    all_to_all x2, waiting for transfers between devices, exchange(): return lax.all_to_all(x, EXPERT, split_axis=0, concat_axis=0, tiled=True)  43.6 us
    pallas_call x1, Pallas kernels, expert_ffn(): pl.pallas_call(ffn_kernel, in_specs=[NEAR] + [FAR] * 3, out_specs=FAR, ou...  12.6 us
    all_to_all x2, starting transfers between devices, exchange(): return lax.all_to_all(x, EXPERT, split_axis=0, concat_axis=0, tiled=True)  9.96 us
    pallas_call x1, Pallas kernels, route(): pl.pallas_call(route_kernel, in_specs=[FAR] * 3, out_specs=FAR, out_shape...  4.59 us
    pallas_call x1, Pallas kernels, mix(): pl.pallas_call(mix_kernel, in_specs=[NEAR, FAR] + [SCALARS] * 2 + [NEAR]...  3.85 us
  transfers between devices with their start and end apart: 2, of which 2 were waited for; matrix products, arithmetic and copies ran while one was open for 0% of the time, Pallas kernels for 3%

profile of v2, /device:TPU:1, one launch (start us, length us, event | category | flops | bytes accessed | tf_op | source)
XLA Modules:
  0.0 138.5 jit_solution(2637997551748582028)
XLA Ops:
  0.6 4.6 %route.1 = bf16[128,96,128]{2,1,0:T(8,128)(2,1)} custom-call(bf16[128,4096]{1,0:T(8,128)(2,1)} %tok_ref.3, f32[1,4096]{1,0:T(1,128)} %bitcast.17, s32[2,128]{1,0:T(2,128)} %bitcast.19), custom_call_target="tpu_custom_call" | custom-call | tf_op jit(solution)/shard_map/route/pallas_call | solution.py:134
  5.2 52.7 %all_to_all.15 = bf16[128,96,128]{2,1,0:T(8,128)(2,1)S(1)} all-to-all(bf16[128,96,128]{2,1,0:T(8,128)(2,1)} %route.1), channel_id=1, replica_groups=mesh['expert_0'=4,'expert_1'=4,'expert_2'=4,'expert_3'=2] {'expert_0','e..., dimensions={0} | all-to-all | bytes 6291456 | tf_op jit(solution)/shard_map/all_to_all | solution.py:367
  57.9 12.6 %ffn.1 = bf16[384,32,128]{2,1,0:T(8,128)(2,1)} custom-call(bf16[384,32,128]{2,1,0:T(8,128)(2,1)S(1)} %bitcast.16, bf16[1,4096,768]{2,1,0:T(8,128)(2,1)} %gate_ref.1, bf16[1,4096,768]{2,1,0:T(8,128)(2,1)} %up_ref.1, bf16[1,768,4096]{2,1,0:T(8,128)(2,1)} %down_ref.1), custom_call_target="tpu_custom_call" | custom-call | flops 7247757312 | bytes 25165824 | tf_op jit(solution)/shard_map/ffn/pallas_call | solution.py:255
  70.5 0.0 copy-start.6
  70.6 0.0 copy-start.1
  70.6 0.0 copy-start.2
  70.6 5.1 %all-to-all-start.1 = ((bf16[128,96,128]{2,1,0:T(8,128)(2,1)}), bf16[128,96,128]{2,1,0:T(8,128)(2,1)S(1)}, u32[]{:S(2)}, u32[]{:S(2)}) async-start(bf16[128,96,128]{2,1,0:T(8,128)(2,1)} %bitcast.23), calls=%async_computation.1 | async-start | bytes 6291456 | tf_op jit(solution)/shard_map/all_to_all | solution.py:367
  75.6 0.0 copy-done.6
  75.7 0.0 copy-done.1
  75.7 0.0 copy-done.2
  75.7 0.0 copy-start
  75.7 1.2 copy-done
  76.9 0.0 copy-start.5
  76.9 1.2 copy-done.5
  78.1 0.0 copy-start.3
  78.1 0.0 copy-start.4
  78.1 2.2 %gate.1 = (f32[8,128]{1,0:T(8,128)S(1)}, s32[8,128]{1,0:T(8,128)S(1)}, bf16[128,32,128]{2,1,0:T(8,128)(2,1)}) custom-call(bf16[128,4096]{1,0:T(8,128)(2,1)S(1)} %copy-done, f32[1,4096]{1,0:T(1,128)S(1)} %bitcast.18, bf16[4096,128]{1,0:T(8,128)(2,1)S(1)} %copy-done.5, s32[2,128]{1,0:T(2,128)S(1)} %bitcast.20), custom_call_target="tpu_custom_call" | custom-call | flops 10000000000 | bytes 4194304 | tf_op jit(solution)/shard_map/gate/pallas_call | solution.py:186
  80.3 36.7 %all-to-all-done.1 = bf16[128,96,128]{2,1,0:T(8,128)(2,1)S(1)} async-done(((bf16[128,96,128]{2,1,0:T(8,128)(2,1)}), bf16[128,96,128]{2,1,0:T(8,128)(2,1)S(1)}, u32[]{:S(2)}, u32[]{:S(2)}) %all-to-all-start.1) | async-done | bytes 3145760 | tf_op jit(solution)/shard_map/all_to_all | solution.py:367
  116.9 0.0 copy-done.3
  117.0 0.0 copy-done.4
  117.0 3.9 %mix.1 = (bf16[128,32,128]{2,1,0:T(8,128)(2,1)}, f32[1,128]{1,0:T(1,128)}, f32[128,128]{1,0:T(8,128)}) custom-call(bf16[384,32,128]{2,1,0:T(8,128)(2,1)S(1)} %bitcast.15, bf16[128,32,128]{2,1,0:T(8,128)(2,1)} %get-tuple-element.9.token_ref, f32[8,128]{1,0:T(8,128)S(1)} %get-tuple-element.10.gates_ref, s32[8,128]{1,0:T(8,128)S(1)} %get-tuple-element.11.where_ref, ...), custom_call_target="tpu_custom_call" | custom-call | tf_op jit(solution)/shard_map/mix/pallas_call | solution.py:320
  120.8 4.9 %all-to-all-start.2 = ((f32[128,1,128]{2,1,0:T(1,128)}), f32[128,1,128]{2,1,0:T(1,128)S(1)}, u32[]{:S(2)}, u32[]{:S(2)}) async-start(f32[128,1,128]{2,1,0:T(1,128)} %bitcast.10), calls=%async_computation.2 | async-start | bytes 131072 | tf_op jit(solution)/shard_map/all_to_all | solution.py:367
  125.7 2.7 %widen.1 = bf16[128,4096]{1,0:T(8,128)(2,1)} custom-call(bf16[128,32,128]{2,1,0:T(8,128)(2,1)} %get-tuple-element.12.tall_ref), custom_call_target="tpu_custom_call" | custom-call | flops 10000000000 | bytes 2097152 | tf_op jit(solution)/shard_map/widen/pallas_call | solution.py:355
  128.4 6.9 %all-to-all-done.2 = f32[128,1,128]{2,1,0:T(1,128)S(1)} async-done(((f32[128,1,128]{2,1,0:T(1,128)}), f32[128,1,128]{2,1,0:T(1,128)S(1)}, u32[]{:S(2)}, u32[]{:S(2)}) %all-to-all-start.2) | async-done | bytes 65568 | tf_op jit(solution)/shard_map/all_to_all | solution.py:367
  135.3 0.2 reduce_sum.9
  135.5 0.6 fusion
  (1 shorter events, 0.0 us)
Async XLA Ops:
  70.5 5.1 %copy-start.6 = (bf16[4096]{0:T(1024)(128)(2,1)S(1)}, bf16[4096]{0:T(1024)(128)(2,1)}, u32[]{:S(2)}) copy-start(bf16[4096]{0:T(1024)(128)(2,1)} %param.17) | copy-start | bytes 24580
  70.6 5.1 %copy-start.1 = (f32[4096]{0:T(1024)S(1)}, f32[4096]{0:T(1024)}, u32[]{:S(2)}) copy-start(f32[4096]{0:T(1024)} %param.11) | copy-start | bytes 49156
  70.6 5.1 %copy-start.2 = (s32[128,2]{0,1:T(2,128)S(1)}, s32[128,2]{0,1:T(2,128)}, u32[]{:S(2)}) copy-start(s32[128,2]{0,1:T(2,128)} %param.13) | copy-start | bytes 3076
  70.6 46.4 %all-to-all-start.1 = ((bf16[128,96,128]{2,1,0:T(8,128)(2,1)}), bf16[128,96,128]{2,1,0:T(8,128)(2,1)S(1)}, u32[]{:S(2)}, u32[]{:S(2)}) async-start(bf16[128,96,128]{2,1,0:T(8,128)(2,1)} %bitcast.23), calls=%async_computation.1 | async-start | bytes 6291456 | tf_op jit(solution)/shard_map/all_to_all | solution.py:367
  75.7 1.2 copy-start
  76.9 1.2 copy-start.5
  78.1 38.8 %copy-start.3 = (s32[128]{0:T(128)S(1)}, s32[128]{0:T(128)}, u32[]{:S(2)}) copy-start(s32[128]{0:T(128)} %param.18) | copy-start | bytes 1540
  78.1 38.8 %copy-start.4 = (f32[128]{0:T(128)S(1)}, f32[128]{0:T(128)}, u32[]{:S(2)}) copy-start(f32[128]{0:T(128)} %param.19) | copy-start | bytes 1540
  120.8 14.5 %all-to-all-start.2 = ((f32[128,1,128]{2,1,0:T(1,128)}), f32[128,1,128]{2,1,0:T(1,128)S(1)}, u32[]{:S(2)}, u32[]{:S(2)}) async-start(f32[128,1,128]{2,1,0:T(1,128)} %bitcast.10), calls=%async_computation.2 | async-start | bytes 131072 | tf_op jit(solution)/shard_map/all_to_all | solution.py:367

commit v3 on v2

v3 whole, which is shorter than its diff:
```python
import jax
import jax.numpy as jnp
from jax import lax
from jax.experimental import pallas as pl
from jax.experimental.pallas import tpu as pltpu
from jax.sharding import Mesh
from jax.sharding import PartitionSpec as P

EXPERT = ("expert_0", "expert_1", "expert_2", "expert_3")
F32 = jnp.float32
BF16 = jnp.bfloat16
I32 = jnp.int32
LANES = 128
SLOTS = 3
ROWS = 16
CHUNKS = 4
MIB = 1024 * 1024
NEAR = pl.BlockSpec(memory_space=pltpu.VMEM)
SCALARS = pl.BlockSpec(memory_space=pltpu.SMEM)
FAR = pl.BlockSpec(memory_space=pltpu.HBM)


def params(mib):
    return pltpu.CompilerParams(vmem_limit_bytes=mib * MIB)


def cost(flops, moved):
    return pl.CostEstimate(flops=flops, transcendentals=0, bytes_accessed=moved)


def kept(x):
    return pltpu.with_memory_space_constraint(x, pltpu.VMEM)


def far(x):
    return pltpu.with_memory_space_constraint(x, pltpu.HBM)


def start_all(pairs, sems):
    copies = [pltpu.make_async_copy(src, dst, sems.at[i]) for i, (src, dst) in enumerate(pairs)]
    for copy in copies:
        copy.start()
    return copies


def pieces_of(count, pieces):
    size = count // pieces
    return [pl.ds(i * size, size) for i in range(pieces)]


def iota(shape, dim):
    return lax.broadcasted_iota(I32, shape, dim)


def to_row(column):
    count = column.shape[0]
    spread = jnp.where(iota((count, count), 0) == iota((count, count), 1), column, jnp.zeros_like(column))
    return jnp.sum(spread, axis=0, keepdims=True)


def slots_of(ids_ref, experts):
    count = ids_ref.shape[1]
    hits = [iota((experts, count), 0) == ids_ref[k:k + 1, :] for k in range(2)]
    named = jnp.where(hits[0] | hits[1], 1.0, 0.0).astype(BF16)
    before = jnp.where(iota((count, count), 0) < iota((count, count), 1), 1.0, 0.0).astype(BF16)
    rank = jnp.dot(named, before, preferred_element_type=F32)
    return hits, rank


def norm(wide, gain):
    inverse = lax.rsqrt(jnp.mean(wide * wide, axis=1, keepdims=True) + 1e-05)
    return (wide * inverse * gain).astype(BF16)


def route_kernel(
    tok_ref, gain_ref, ids_ref, out_ref,
    near_ref, gain_near, ids_near, tall_ref, piece_ref, index_ref, index_smem, sems, out_sems, index_sem,
):
    count, width = tok_ref.shape
    parts = width // LANES
    experts = out_ref.shape[0]
    copies = start_all(
        [(ids_ref, ids_near), (gain_ref, gain_near)]
        + [(tok_ref.at[rows], near_ref.at[rows]) for rows in pieces_of(count, CHUNKS)],
        sems,
    )
    copies[0].wait()
    hits, rank = slots_of(ids_near, experts)
    named = hits[0] | hits[1]
    token = (iota((8, count), 1) - count).astype(F32).astype(BF16)
    for s in range(SLOTS):
        chosen = jnp.where(named & (rank == s), 1.0, 0.0).astype(BF16)
        source = lax.dot_general(token, chosen, (((1,), (1,)), ((), ())), preferred_element_type=F32)
        index_ref[s:s + 1, :] = source[0:1].astype(I32) + count
    index_ref[SLOTS:, :] = jnp.zeros((8 - SLOTS, experts), I32)
    index_copy = pltpu.make_async_copy(index_ref, index_smem, index_sem)
    index_copy.start()
    tall_ref[count] = jnp.zeros((parts, LANES), BF16)
    copies[1].wait()
    gain = gain_near[...]
    chunk = count // CHUNKS
    for c in range(CHUNKS):
        copies[2 + c].wait()

        def norm_rows(step, carry, c=c):
            start = pl.multiple_of(c * chunk + step * ROWS, ROWS)
            normed = norm(near_ref[pl.ds(start, ROWS), :].astype(F32), gain)
            tall_ref[pl.ds(start, ROWS)] = normed.astype(F32).reshape(ROWS, parts, LANES).astype(BF16)
            return carry

        lax.fori_loop(0, chunk // ROWS, norm_rows, 0)
    index_copy.wait()
    chunk = experts // CHUNKS
    sent = []
    for c, rows in enumerate(pieces_of(experts, CHUNKS)):
        def send(step, carry, c=c):
            for i in range(4):
                e = c * chunk + step * 4 + i
                for s in range(SLOTS):
                    piece_ref[e, s * parts:(s + 1) * parts] = tall_ref[index_smem[s, e]]
            return carry

        lax.fori_loop(0, chunk // 4, send, 0)
        sent.append(pltpu.make_async_copy(piece_ref.at[rows], out_ref.at[rows], out_sems.at[c]))
        sent[c].start()
    for copy in sent:
        copy.wait()


def route(tokens, norm_gain, ids, experts):
    count, width = tokens.shape
    parts = width // LANES
    pieces = (experts, SLOTS * parts, LANES)
    return pl.pallas_call(
        route_kernel,
        in_specs=[FAR] * 3,
        out_specs=FAR,
        out_shape=pltpu.HBM(pieces, BF16),
        scratch_shapes=[
            pltpu.VMEM((count, width), BF16),
            pltpu.VMEM(norm_gain.shape, F32),
            pltpu.VMEM(ids.shape, I32),
            pltpu.VMEM((count + 1, parts, LANES), BF16),
            pltpu.VMEM(pieces, BF16),
            pltpu.VMEM((8, experts), I32),
            pltpu.SMEM((8, experts), I32),
            pltpu.SemaphoreType.DMA((2 + CHUNKS,)),
            pltpu.SemaphoreType.DMA((CHUNKS,)),
            pltpu.SemaphoreType.DMA(()),
        ],
        compiler_params=params(16),
        name="route",
    )(far(tokens), far(norm_gain), far(ids))


def gate_kernel(
    *refs,
):
    inputs, (gates_ref, where_ref, base_ref, out_ref), scratch = refs[:6], refs[6:10], refs[10:]
    tok_ref, gain_ref, router_ref, ids_ref, weight_ref, down_ref, normed_ref, score_ref, sems = scratch
    for copy in start_all(zip(inputs, scratch[:6]), sems):
        copy.wait()
    count, width = tok_ref.shape
    experts = router_ref.shape[1]
    gain = gain_ref[...]
    weight = weight_ref[...]

    def norm_rows(step, carry):
        start = pl.multiple_of(step * ROWS, ROWS)
        wide = tok_ref[pl.ds(start, ROWS), :].astype(F32)
        normed_ref[pl.ds(start, ROWS), :] = norm(wide, gain)
        score_ref[pl.ds(start, ROWS), :] = jnp.sum(wide * weight, axis=1, keepdims=True)
        return carry

    lax.fori_loop(0, count // ROWS, norm_rows, 0)
    base_ref[...] = to_row(score_ref[...])
    hits, rank = slots_of(ids_ref, experts)
    logits = jnp.transpose(jnp.dot(normed_ref[...], router_ref[...], preferred_element_type=F32))
    scores = []
    where_ref[...] = jnp.zeros(where_ref.shape, I32)
    gates_ref[...] = jnp.zeros(gates_ref.shape, F32)
    for k in range(2):
        slot = jnp.sum(jnp.where(hits[k], rank, 0.0), axis=0, keepdims=True).astype(I32)
        where_ref[k:k + 1, :] = ids_ref[k:k + 1, :] * SLOTS + slot
        scores.append(jnp.sum(jnp.where(hits[k], logits, 0.0), axis=0, keepdims=True))
    gates_ref[0:1, :] = jax.nn.sigmoid(scores[0] - scores[1])
    gates_ref[1:2, :] = jax.nn.sigmoid(scores[1] - scores[0])

    def score_rows(step, carry):
        start = pl.multiple_of(step * ROWS, ROWS)
        products = down_ref[0, pl.ds(start, ROWS), :].astype(F32) * weight
        scored = jnp.broadcast_to(jnp.sum(products, axis=1, keepdims=True), (ROWS, LANES))
        high = scored.astype(BF16)
        out_ref[pl.ds(start, ROWS), 0:LANES] = high
        out_ref[pl.ds(start, ROWS), LANES:] = (scored - high.astype(F32)).astype(BF16)
        return carry

    lax.fori_loop(0, down_ref.shape[1] // ROWS, score_rows, 0)


def gate(tokens, norm_gain, router_weight, ids, weight, down_proj):
    count, width = tokens.shape
    inputs = (tokens, norm_gain, router_weight, ids, weight, down_proj)
    return pl.pallas_call(
        gate_kernel,
        in_specs=[FAR] * 6,
        out_specs=[NEAR] * 4,
        out_shape=[
            jax.ShapeDtypeStruct((8, count), F32),
            jax.ShapeDtypeStruct((8, count), I32),
            jax.ShapeDtypeStruct((1, count), F32),
            jax.ShapeDtypeStruct((down_proj.shape[1], 2 * LANES), BF16),
        ],
        scratch_shapes=[pltpu.VMEM(x.shape, x.dtype) for x in inputs]
        + [pltpu.VMEM((count, width), BF16), pltpu.VMEM((count, 1), F32), pltpu.SemaphoreType.DMA((6,))],
        compiler_params=params(24),
        cost_estimate=cost(10**10, 10 * MIB),
        name="gate",
    )(*[far(x) for x in inputs])


def up_kernel(
    in_ref, gate_ref, up_ref, score_ref, hidden_out, values_ref,
    gate_near, up_near, score_near, wide_ref, hidden_ref, sems, out_sem,
):
    sources = in_ref.shape[0]
    width, hidden = gate_near.shape
    parts = width // LANES
    tiles = [slice(start, start + 256) for start in range(0, hidden, 256)]
    pairs = []
    for tile in tiles:
        pairs.append((gate_ref.at[0, :, tile], gate_near.at[:, tile]))
        pairs.append((up_ref.at[0, :, tile], up_near.at[:, tile]))
    copies = start_all(pairs + [(score_ref, score_near)], sems)
    for s in range(SLOTS):
        def widen(i, carry, s=s):
            start = pl.multiple_of(i * ROWS, ROWS)
            tall = in_ref[pl.ds(start, ROWS), s * parts:(s + 1) * parts].astype(F32)
            wide_ref[pl.ds(s * sources + start, ROWS), :] = tall.reshape(ROWS, width).astype(BF16)
            return carry

        lax.fori_loop(0, sources // ROWS, widen, 0)
    for i, tile in enumerate(tiles):
        copies[2 * i].wait()
        copies[2 * i + 1].wait()
        x = wide_ref[...]
        gated = jnp.dot(x, gate_near[:, tile], preferred_element_type=F32)
        upped = jnp.dot(x, up_near[:, tile], preferred_element_type=F32)
        hidden_ref[:, tile] = (jax.nn.silu(gated) * upped).astype(BF16)
    sent = pltpu.make_async_copy(hidden_ref, hidden_out, out_sem)
    sent.start()
    copies[-1].wait()
    both = jnp.dot(hidden_ref[...], score_near[...], preferred_element_type=F32)
    both = both[:, :LANES] + both[:, LANES:]
    lane = iota((sources, LANES), 1)
    by_slot = jnp.zeros((sources, LANES), F32)
    for s in range(SLOTS):
        by_slot = jnp.where(lane == s, both[s * sources:(s + 1) * sources], by_slot)
    values_ref[...] = by_slot
    sent.wait()


def expert_up(received, gate_proj, up_proj, scores):
    sources = received.shape[0]
    rows = SLOTS * sources
    _, width, hidden = gate_proj.shape
    return pl.pallas_call(
        up_kernel,
        in_specs=[NEAR] + [FAR] * 3,
        out_specs=[FAR, NEAR],
        out_shape=[pltpu.HBM((rows, hidden), BF16), jax.ShapeDtypeStruct((sources, LANES), F32)],
        scratch_shapes=[
            pltpu.VMEM((width, hidden), BF16),
            pltpu.VMEM((width, hidden), BF16),
            pltpu.VMEM(scores.shape, BF16),
            pltpu.VMEM((rows, width), BF16),
            pltpu.VMEM((rows, hidden), BF16),
            pltpu.SemaphoreType.DMA((2 * (hidden // 256) + 1,)),
            pltpu.SemaphoreType.DMA(()),
        ],
        compiler_params=params(40),
        cost_estimate=cost(4 * rows * width * hidden, 18 * MIB),
        name="expert_up",
    )(kept(received), far(gate_proj), far(up_proj), far(scores))


def down_kernel(hidden_ref, down_ref, out_ref, hidden_near, down_near, wide_ref, piece_ref, sems, out_sems):
    hidden, width = down_near.shape
    sources = out_ref.shape[0]
    parts = width // LANES
    tiles = [slice(start, start + 1024) for start in range(0, width, 1024)]
    copies = start_all(
        [(hidden_ref, hidden_near)] + [(down_ref.at[0, :, tile], down_near.at[:, tile]) for tile in tiles], sems
    )
    copies[0].wait()
    for i, tile in enumerate(tiles):
        copies[1 + i].wait()
        for start in range(tile.start, tile.stop, 512):
            at = slice(start, start + 512)
            wide = jnp.dot(hidden_near[...], down_near[:, at], preferred_element_type=F32)
            wide_ref[:, at] = wide.astype(BF16)
    pieces = out_sems.shape[0]
    chunk = sources // pieces
    sent = []
    for p, piece in enumerate(pieces_of(sources, pieces)):
        for s in range(SLOTS):
            def heighten(i, carry, p=p, s=s):
                start = pl.multiple_of(p * chunk + i * ROWS, ROWS)
                wide = wide_ref[pl.ds(s * sources + start, ROWS), :].astype(F32)
                tall = wide.reshape(ROWS, parts, LANES).astype(BF16)
                piece_ref[pl.ds(start, ROWS), s * parts:(s + 1) * parts] = tall
                return carry

            lax.fori_loop(0, chunk // ROWS, heighten, 0)
        sent.append(pltpu.make_async_copy(piece_ref.at[piece], out_ref.at[piece], out_sems.at[p]))
        sent[p].start()
    for copy in sent:
        copy.wait()


def expert_down(hidden_rows, down_proj):
    rows, hidden = hidden_rows.shape
    width = down_proj.shape[2]
    shape = (rows // SLOTS, SLOTS * (width // LANES), LANES)
    return pl.pallas_call(
        down_kernel,
        in_specs=[FAR] * 2,
        out_specs=FAR,
        out_shape=pltpu.HBM(shape, BF16),
        scratch_shapes=[
            pltpu.VMEM((rows, hidden), BF16),
            pltpu.VMEM((hidden, width), BF16),
            pltpu.VMEM((rows, width), BF16),
            pltpu.VMEM(shape, BF16),
            pltpu.SemaphoreType.DMA((1 + width // 1024,)),
            pltpu.SemaphoreType.DMA((4,)),
        ],
        compiler_params=params(24),
        cost_estimate=cost(2 * rows * width * hidden, 12 * MIB),
        name="expert_down",
    )(far(hidden_rows), far(down_proj))


def value_kernel(part_ref, ids_ref, gates_ref, base_ref, target_ref, recency_ref, values_ref, sums_ref):
    experts = part_ref.shape[0]
    hits, rank = slots_of(ids_ref, experts)
    total = base_ref[...]
    part = jnp.zeros(rank.shape, F32)
    for s in range(SLOTS):
        part = jnp.where(rank == s, part_ref[:, s:s + 1], part)
    for k in range(2):
        picked = jnp.sum(jnp.where(hits[k], part, 0.0), axis=0, keepdims=True)
        total = total + gates_ref[k:k + 1, :] * picked
    values = jnp.tanh(total)
    values_ref[...] = values
    error = values - target_ref[...].astype(F32)
    recency = recency_ref[...]
    weighted = jnp.sum(recency * error * error, axis=1, keepdims=True)
    weights = jnp.sum(recency, axis=1, keepdims=True)
    lane = iota(sums_ref.shape, 1)
    sums_ref[...] = jnp.where(lane == 0, weighted, jnp.where(lane == 1, weights, 0.0))


def value(part, ids, gates, base, target, recency):
    return pl.pallas_call(
        value_kernel,
        in_specs=[NEAR] * 6,
        out_specs=[NEAR] * 2,
        out_shape=[jax.ShapeDtypeStruct(base.shape, F32), jax.ShapeDtypeStruct((1, LANES), F32)],
        compiler_params=params(8),
        cost_estimate=cost(10**9, MIB),
        name="value",
    )(part, ids, gates, base, target, recency)


def mix_kernel(
    back_ref, token_ref, gates_ref, where_ref, mixed_ref, near_ref, out_near, sum_ref, sems, out_sems
):
    count, width = token_ref.shape
    parts = width // LANES
    rows = pieces_of(count, CHUNKS)
    copies = start_all([(token_ref.at[r], near_ref.at[r]) for r in rows], sems)
    chunk = count // CHUNKS
    sent = []
    for c in range(CHUNKS):
        copies[c].wait()

        def mix_rows(step, carry, c=c):
            start = pl.multiple_of(c * chunk + step * ROWS, ROWS)
            for i in range(ROWS):
                t = start + i
                first = gates_ref[0, t] * back_ref[where_ref[0, t]].astype(F32)
                sum_ref[i] = first + gates_ref[1, t] * back_ref[where_ref[1, t]].astype(F32)
            update = sum_ref[...].reshape(ROWS, width)
            mixed = near_ref[pl.ds(start, ROWS), :].astype(F32) + update
            out_near[pl.ds(start, ROWS), :] = mixed.astype(BF16)
            return carry

        lax.fori_loop(0, chunk // ROWS, mix_rows, 0)
        sent.append(pltpu.make_async_copy(out_near.at[rows[c]], mixed_ref.at[rows[c]], out_sems.at[c]))
        sent[c].start()
    for copy in sent:
        copy.wait()


def mix(back, tokens, gates, where):
    count, width = tokens.shape
    return pl.pallas_call(
        mix_kernel,
        in_specs=[NEAR, FAR] + [SCALARS] * 2,
        out_specs=FAR,
        out_shape=pltpu.HBM(tokens.shape, BF16),
        scratch_shapes=[
            pltpu.VMEM(tokens.shape, BF16),
            pltpu.VMEM(tokens.shape, BF16),
            pltpu.VMEM((ROWS, width // LANES, LANES), F32),
            pltpu.SemaphoreType.DMA((CHUNKS,)),
            pltpu.SemaphoreType.DMA((CHUNKS,)),
        ],
        compiler_params=params(16),
        name="mix",
    )(kept(back), far(tokens), gates, where)


def everywhere(x):
    for axis in EXPERT[::-1]:
        x = lax.psum(x, axis)
    return x


def exchange(x):
    return lax.all_to_all(x, EXPERT, split_axis=0, concat_axis=0, tiled=True)


def body(
    tokens,
    norm_gain,
    router_weight,
    expert_ids,
    gate_proj,
    up_proj,
    down_proj,
    value_weight,
    value_target,
    recency,
):
    count, width = tokens.shape
    experts = router_weight.shape[1]
    parts = width // LANES
    ids = expert_ids.T
    gain = norm_gain.reshape(1, width)
    weight = value_weight.reshape(1, width).astype(F32)
    received = exchange(route(tokens, gain, ids, experts))
    gates, where, base, scores = gate(tokens, gain, router_weight, ids, weight, down_proj)
    hidden, scored = expert_up(received, gate_proj, up_proj, scores)
    part = exchange(scored.reshape(experts, 1, LANES)).reshape(experts, LANES)
    back = exchange(expert_down(hidden, down_proj))
    values, sums = value(
        part, ids, gates, base, value_target.reshape(1, count), recency.reshape(1, count)
    )
    total = everywhere(sums)
    mixed = mix(back.reshape(experts * SLOTS, parts, LANES), tokens, gates, where)
    return (mixed, values.reshape(count), total[0, 0] / total[0, 1])


def solution(mesh):
    finer = Mesh(mesh.devices.reshape(4, 4, 4, 2), EXPERT)
    in_specs = (
        P(EXPERT, None),
        P(),
        P(),
        P(EXPERT, None),
        P(EXPERT, None, None),
        P(EXPERT, None, None),
        P(EXPERT, None, None),
        P(),
        P(EXPERT),
        P(EXPERT),
    )
    out_specs = (P(EXPERT, None), P(EXPERT), P())
    return jax.shard_map(body, mesh=finer, in_specs=in_specs, out_specs=out_specs, check_vma=False)
```

time: 139 us -> 155 us (1.12)
  the two profiles are of different devices: /device:TPU:1 before, /device:TPU:32 now
where the time goes in v3:
time: 155 us
  blocking collectives  59.5 us (38%)
  Pallas kernels  36.6 us (24%)
  waiting for transfers between devices  29.7 us (19%)
  starting transfers between devices  23.9 us (15%)
  between operations  3.24 us (2%)
    psum x4, blocking collectives, everywhere(): x = lax.psum(x, axis)  59.5 us
    all_to_all x3, waiting for transfers between devices, exchange(): return lax.all_to_all(x, EXPERT, split_axis=0, concat_axis=0, tiled=True)  29.7 us
    all_to_all x3, starting transfers between devices, exchange(): return lax.all_to_all(x, EXPERT, split_axis=0, concat_axis=0, tiled=True)  23.9 us
    pallas_call x1, Pallas kernels, gate(): pl.pallas_call(gate_kernel, in_specs=[FAR] * 6, out_specs=[NEAR] * 4, out...  11.3 us
    pallas_call x1, Pallas kernels, expert_up(): pl.pallas_call(up_kernel, in_specs=[NEAR] + [FAR] * 3, out_specs=[FAR, NE...  9.28 us
    pallas_call x1, Pallas kernels, expert_down(): pl.pallas_call(down_kernel, in_specs=[FAR] * 2, out_specs=FAR, out_shape=...  7.16 us
    pallas_call x1, Pallas kernels, route(): pl.pallas_call(route_kernel, in_specs=[FAR] * 3, out_specs=FAR, out_shape...  4.62 us
    pallas_call x1, Pallas kernels, mix(): pl.pallas_call(mix_kernel, in_specs=[NEAR, FAR] + [SCALARS] * 2, out_spec...  3.49 us
  transfers between devices with their start and end apart: 3, of which 2 were waited for; matrix products, arithmetic and copies ran while one was open for 1% of the time, Pallas kernels for 12%

profile of v3, /device:TPU:32, one launch (start us, length us, event | category | flops | bytes accessed | tf_op | source)
XLA Modules:
  0.0 154.8 jit_solution(3863368816757205070)
XLA Ops:
  0.6 4.6 %route.1 = bf16[128,96,128]{2,1,0:T(8,128)(2,1)} custom-call(bf16[128,4096]{1,0:T(8,128)(2,1)} %token_ref.1, f32[1,4096]{1,0:T(1,128)} %bitcast.19, s32[2,128]{1,0:T(2,128)} %bitcast.14), custom_call_target="tpu_custom_call" | custom-call | tf_op jit(solution)/shard_map/route/pallas_call | solution.py:134
  5.3 0.0 copy-start.4
  5.3 10.2 %all-to-all-start = ((bf16[128,96,128]{2,1,0:T(8,128)(2,1)}), bf16[128,96,128]{2,1,0:T(8,128)(2,1)S(1)}, u32[]{:S(2)}, u32[]{:S(2)}) async-start(bf16[128,96,128]{2,1,0:T(8,128)(2,1)} %route.1), calls=%async_computation | async-start | bytes 6291456 | tf_op jit(solution)/shard_map/all_to_all | solution.py:432
  15.5 0.0 copy-done.4
  15.5 0.6 convert_element_type.7
  16.1 11.3 %gate.1 = (f32[8,128]{1,0:T(8,128)S(1)}, s32[8,128]{1,0:T(8,128)S(1)}, f32[1,128]{1,0:T(1,128)S(1)}, bf16[768,256]{1,0:T(8,128)(2,1)S(1)}) custom-call(bf16[128,4096]{1,0:T(8,128)(2,1)} %token_ref.1, f32[1,4096]{1,0:T(1,128)} %bitcast.20, bf16[4096,128]{1,0:T(8,128)(2,1)} %refs_2_.1, s32[2,128]{1,0:T(2,128)} %bitcast.15, f32[1,4096]{1,0:T(1,128)} %bitcast.21, ...), custom_call_target="tpu_custom_call" | custom-call | flops 10000000000 | bytes 10485760 | tf_op jit(solution)/shard_map/gate/pallas_call | solution.py:204
  27.4 0.0 copy-start.3
  27.4 0.7 copy-done.3
  28.2 28.1 %all-to-all-done.in_ref = bf16[128,96,128]{2,1,0:T(8,128)(2,1)S(1)} async-done(((bf16[128,96,128]{2,1,0:T(8,128)(2,1)}), bf16[128,96,128]{2,1,0:T(8,128)(2,1)S(1)}, u32[]{:S(2)}, u32[]{:S(2)}) %all-to-all-start) | async-done | bytes 3145760 | tf_op jit(solution)/shard_map/all_to_all | solution.py:432
  56.3 9.3 %expert_up.1 = (bf16[384,768]{1,0:T(8,128)(2,1)}, f32[128,128]{1,0:T(8,128)}) custom-call(bf16[128,96,128]{2,1,0:T(8,128)(2,1)S(1)} %all-to-all-done.in_ref, bf16[1,4096,768]{2,1,0:T(8,128)(2,1)} %gate_ref.1, bf16[1,4096,768]{2,1,0:T(8,128)(2,1)} %up_ref.1, bf16[768,256]{1,0:T(8,128)(2,1)} %copy-done.3), custom_call_target="tpu_custom_call" | custom-call | flops 4831838208 | bytes 18874368 | tf_op jit(solution)/shard_map/expert_up/pallas_call | solution.py:267
  65.6 5.5 %all-to-all-start.2 = ((f32[128,1,128]{2,1,0:T(1,128)}), f32[128,1,128]{2,1,0:T(1,128)S(1)}, u32[]{:S(2)}, u32[]{:S(2)}) async-start(f32[128,1,128]{2,1,0:T(1,128)} %bitcast.5), calls=%async_computation.2 | async-start | bytes 131072 | tf_op jit(solution)/shard_map/all_to_all | solution.py:432
  71.0 7.2 %expert_down.1 = bf16[128,96,128]{2,1,0:T(8,128)(2,1)} custom-call(bf16[384,768]{1,0:T(8,128)(2,1)} %get-tuple-element.12.hidden_ref, bf16[1,768,4096]{2,1,0:T(8,128)(2,1)} %down_ref.1), custom_call_target="tpu_custom_call" | custom-call | flops 2415919104 | bytes 12582912 | tf_op jit(solution)/shard_map/expert_down/pallas_call | solution.py:325
  78.2 0.0 copy-start
  78.2 0.0 copy-start.1
  78.2 0.0 copy-start.2
  78.2 1.6 %all-to-all-done.2 = f32[128,1,128]{2,1,0:T(1,128)S(1)} async-done(((f32[128,1,128]{2,1,0:T(1,128)}), f32[128,1,128]{2,1,0:T(1,128)S(1)}, u32[]{:S(2)}, u32[]{:S(2)}) %all-to-all-start.2) | async-done | bytes 65568 | tf_op jit(solution)/shard_map/all_to_all | solution.py:432
  79.8 8.2 %all-to-all-start.1 = ((bf16[128,96,128]{2,1,0:T(8,128)(2,1)}), bf16[128,96,128]{2,1,0:T(8,128)(2,1)S(1)}, u32[]{:S(2)}, u32[]{:S(2)}) async-start(bf16[128,96,128]{2,1,0:T(8,128)(2,1)} %expert_down.1), calls=%async_computation.1 | async-start | bytes 6291456 | tf_op jit(solution)/shard_map/all_to_all | solution.py:432
  88.0 0.0 copy-done
  88.0 0.0 copy-done.1
  88.0 0.0 copy-done.2
  88.0 0.7 value.1
  88.7 2.4 %psum.28 = f32[1,128]{1,0:T(1,128)S(1)} all-reduce(f32[1,128]{1,0:T(1,128)S(1)} %get-tuple-element.18), channel_id=1, replica_groups=mesh['expert_0'=4,'expert_1'=4,'expert_2'=4,'expert_3'=2] {'expert_3'}, use_global_device_ids=true, to_apply=%region_0.0 | all-reduce | flops 128 | bytes 1024 | tf_op jit(solution)/shard_map/psum | solution.py:427
  91.2 20.6 %psum.29 = f32[1,128]{1,0:T(1,128)S(1)} all-reduce(f32[1,128]{1,0:T(1,128)S(1)} %psum.28), channel_id=1, replica_groups=mesh['expert_0'=4,'expert_1'=4,'expert_2'=4,'expert_3'=2] {'expert_2'}, use_global_device_ids=true, to_apply=%region_1.0 | all-reduce | flops 128 | bytes 1024 | tf_op jit(solution)/shard_map/psum | solution.py:427
  111.8 25.6 %psum.30 = f32[1,128]{1,0:T(1,128)S(1)} all-reduce(f32[1,128]{1,0:T(1,128)S(1)} %psum.29), channel_id=1, replica_groups=mesh['expert_0'=4,'expert_1'=4,'expert_2'=4,'expert_3'=2] {'expert_1'}, use_global_device_ids=true, to_apply=%region_2.0 | all-reduce | flops 128 | bytes 1024 | tf_op jit(solution)/shard_map/psum | solution.py:427
  137.4 10.9 %psum.31 = f32[1,128]{1,0:T(1,128)S(1)} all-reduce(f32[1,128]{1,0:T(1,128)S(1)} %psum.30), channel_id=1, replica_groups=mesh['expert_0'=4,'expert_1'=4,'expert_2'=4,'expert_3'=2] {'expert_0'}, use_global_device_ids=true, to_apply=%region_3.0 | all-reduce | flops 128 | bytes 1024 | tf_op jit(solution)/shard_map/psum | solution.py:427
  148.3 0.6 fusion
  150.2 0.0 all-to-all-done.1
  150.2 3.5 %mix.1 = bf16[128,4096]{1,0:T(8,128)(2,1)} custom-call(bf16[384,32,128]{2,1,0:T(8,128)(2,1)S(1)} %bitcast.12, bf16[128,4096]{1,0:T(8,128)(2,1)} %token_ref.1, f32[8,128]{1,0:T(8,128)S(1)} %get-tuple-element.13.gates_ref, s32[8,128]{1,0:T(8,128)S(1)} %get-tuple-element.14.where_ref), custom_call_target="tpu_custom_call" | custom-call | tf_op jit(solution)/shard_map/mix/pallas_call | solution.py:408
Async XLA Ops:
  5.3 10.3 %copy-start.4 = (bf16[4096]{0:T(1024)(128)(2,1)S(1)}, bf16[4096]{0:T(1024)(128)(2,1)}, u32[]{:S(2)}) copy-start(bf16[4096]{0:T(1024)(128)(2,1)} %param.17) | copy-start | bytes 24580
  5.3 51.0 %all-to-all-start = ((bf16[128,96,128]{2,1,0:T(8,128)(2,1)}), bf16[128,96,128]{2,1,0:T(8,128)(2,1)S(1)}, u32[]{:S(2)}, u32[]{:S(2)}) async-start(bf16[128,96,128]{2,1,0:T(8,128)(2,1)} %route.1), calls=%async_computation | async-start | bytes 6291456 | tf_op jit(solution)/shard_map/all_to_all | solution.py:432
  27.4 0.8 copy-start.3
  65.6 14.3 %all-to-all-start.2 = ((f32[128,1,128]{2,1,0:T(1,128)}), f32[128,1,128]{2,1,0:T(1,128)S(1)}, u32[]{:S(2)}, u32[]{:S(2)}) async-start(f32[128,1,128]{2,1,0:T(1,128)} %bitcast.5), calls=%async_computation.2 | async-start | bytes 131072 | tf_op jit(solution)/shard_map/all_to_all | solution.py:432
  78.2 9.8 %copy-start = (s32[128,2]{0,1:T(2,128)S(1)}, s32[128,2]{0,1:T(2,128)}, u32[]{:S(2)}) copy-start(s32[128,2]{0,1:T(2,128)} %param.13) | copy-start | bytes 3076
  78.2 9.8 %copy-start.1 = (s32[128]{0:T(128)S(1)}, s32[128]{0:T(128)}, u32[]{:S(2)}) copy-start(s32[128]{0:T(128)} %param.18) | copy-start | bytes 1540
  78.2 9.8 %copy-start.2 = (f32[128]{0:T(128)S(1)}, f32[128]{0:T(128)}, u32[]{:S(2)}) copy-start(f32[128]{0:T(128)} %param.19) | copy-start | bytes 1540
  79.8 70.4 %all-to-all-start.1 = ((bf16[128,96,128]{2,1,0:T(8,128)(2,1)}), bf16[128,96,128]{2,1,0:T(8,128)(2,1)S(1)}, u32[]{:S(2)}, u32[]{:S(2)}) async-start(bf16[128,96,128]{2,1,0:T(8,128)(2,1)} %expert_down.1), calls=%async_computation.1 | async-start | bytes 6291456 | tf_op jit(solution)/shard_map/all_to_all | solution.py:432

commit v4 on v2

--- a/solution.py
+++ b/solution.py
@@ -13,10 +13,11 @@
 LANES = 128
 SLOTS = 3
 ROWS = 16
+NORM_ROWS = 32
+BLOCK = 128
 CHUNKS = 4
 MIB = 1024 * 1024
 NEAR = pl.BlockSpec(memory_space=pltpu.VMEM)
-SCALARS = pl.BlockSpec(memory_space=pltpu.SMEM)
 FAR = pl.BlockSpec(memory_space=pltpu.HBM)
 
 
@@ -103,12 +104,12 @@
         copies[2 + c].wait()
 
         def norm_rows(step, carry, c=c):
-            start = pl.multiple_of(c * chunk + step * ROWS, ROWS)
-            normed = norm(near_ref[pl.ds(start, ROWS), :].astype(F32), gain)
-            tall_ref[pl.ds(start, ROWS)] = normed.astype(F32).reshape(ROWS, parts, LANES).astype(BF16)
+            start = pl.multiple_of(c * chunk + step * NORM_ROWS, NORM_ROWS)
+            normed = norm(near_ref[pl.ds(start, NORM_ROWS), :].astype(F32), gain)
+            tall_ref[pl.ds(start, NORM_ROWS)] = normed.astype(F32).reshape(NORM_ROWS, parts, LANES).astype(BF16)
             return carry
 
-        lax.fori_loop(0, chunk // ROWS, norm_rows, 0)
+        lax.fori_loop(0, chunk // NORM_ROWS, norm_rows, 0)
     index_copy.wait()
     chunk = experts // CHUNKS
     sent = []
@@ -230,19 +231,16 @@
         hidden_ref[:, tile] = (jax.nn.silu(gated) * upped).astype(BF16)
     for i in range(len(tiles)):
         copies[2 * len(tiles) + i].wait()
-    for start in range(0, width, 512):
-        tile = slice(start, start + 512)
-        wide_ref[:, tile] = jnp.dot(hidden_ref[...], down_near[:, tile], preferred_element_type=F32).astype(BF16)
-    pieces = out_sems.shape[0]
+    half = width // 2
     sent = []
-    for p, piece in enumerate(pieces_of(rows, pieces)):
-        def heighten(i, carry, p=p):
-            start = pl.multiple_of(p * (rows // pieces) + i * ROWS, ROWS)
-            wide = wide_ref[pl.ds(start, ROWS), :].astype(F32)
-            tall_ref[pl.ds(start, ROWS)] = wide.reshape(ROWS, parts, LANES).astype(BF16)
-            return carry
-
-        lax.fori_loop(0, rows // pieces // ROWS, heighten, 0)
+    for p, start in enumerate(range(0, rows, BLOCK)):
+        piece = slice(start, start + BLOCK)
+        for side in range(2):
+            wide = jnp.dot(
+                hidden_ref[piece, :], down_near[:, side * half:(side + 1) * half], preferred_element_type=F32
+            )
+            tall = wide.reshape(BLOCK, parts // 2, LANES).astype(BF16)
+            tall_ref[piece, side * (parts // 2):(side + 1) * (parts // 2)] = tall
         sent.append(pltpu.make_async_copy(tall_ref.at[piece], out_ref.at[piece], out_sems.at[p]))
         sent[p].start()
     for copy in sent:
@@ -265,9 +263,9 @@
             pltpu.VMEM((rows, hidden), BF16),
             pltpu.VMEM((rows, parts, LANES), BF16),
             pltpu.SemaphoreType.DMA((3 * (hidden // 256),)),
-            pltpu.SemaphoreType.DMA((6,)),
+            pltpu.SemaphoreType.DMA((rows // BLOCK,)),
         ],
-        compiler_params=params(40),
+        compiler_params=params(44),
         cost_estimate=cost(6 * rows * width * hidden, 24 * MIB),
         name="ffn",
     )(kept(received), far(gate_proj), far(up_proj), far(down_proj))
@@ -276,30 +274,34 @@
 def mix_kernel(
     back_ref, token_ref, gates_ref, where_ref, weight_ref, target_ref, recency_ref,
     mixed_ref, values_ref, sums_ref,
-    tall_ref, near_ref, score_ref, sems, out_sems,
+    tall_ref, near_ref, score_ref, gates_smem, where_smem, sems, out_sems,
 ):
     count, parts, _ = token_ref.shape
     rows = pieces_of(count, CHUNKS)
-    copies = start_all([(token_ref.at[r], tall_ref.at[r]) for r in rows], sems)
+    copies = start_all(
+        [(gates_ref, gates_smem), (where_ref, where_smem)] + [(token_ref.at[r], tall_ref.at[r]) for r in rows], sems
+    )
     weight = weight_ref[...]
     chunk = count // CHUNKS
     sent = []
+    copies[0].wait()
+    copies[1].wait()
     for c in range(CHUNKS):
-        copies[c].wait()
+        copies[2 + c].wait()
 
         def mix_rows(step, carry, c=c):
-            for i in range(8):
-                t = c * chunk + step * 8 + i
+            for i in range(16):
+                t = c * chunk + step * 16 + i
                 total = tall_ref[t].astype(F32)
                 for k in range(2):
-                    total = total + gates_ref[k, t] * back_ref[where_ref[k, t]].astype(F32)
+                    total = total + gates_smem[k, t] * back_ref[where_smem[k, t]].astype(F32)
                 mixed = total.astype(BF16)
                 near_ref[t] = mixed
                 scored = mixed.astype(F32) * weight
                 score_ref[t] = jnp.sum(scored.reshape(parts // 8, 8, LANES), axis=0)
             return carry
 
-        lax.fori_loop(0, chunk // 8, mix_rows, 0)
+        lax.fori_loop(0, chunk // 16, mix_rows, 0)
         sent.append(pltpu.make_async_copy(near_ref.at[rows[c]], mixed_ref.at[rows[c]], out_sems.at[c]))
         sent[c].start()
     by_lane = jnp.sum(score_ref[...], axis=1)
@@ -319,23 +321,25 @@
     count, parts, _ = tall.shape
     return pl.pallas_call(
         mix_kernel,
-        in_specs=[NEAR, FAR] + [SCALARS] * 2 + [NEAR] * 3,
+        in_specs=[NEAR, FAR] + [NEAR] * 5,
         out_specs=[FAR] + [NEAR] * 2,
         out_shape=[
             pltpu.HBM(tall.shape, BF16),
-            jax.ShapeDtypeStruct((1, count), F32),
-            jax.ShapeDtypeStruct((devices, LANES), F32),
+            pltpu.VMEM((1, count), F32),
+            pltpu.VMEM((devices, LANES), F32),
         ],
         scratch_shapes=[
             pltpu.VMEM((count, parts, LANES), BF16),
             pltpu.VMEM((count, parts, LANES), BF16),
             pltpu.VMEM((count, 8, LANES), F32),
-            pltpu.SemaphoreType.DMA((CHUNKS,)),
+            pltpu.SMEM(gates.shape, F32),
+            pltpu.SMEM(where.shape, I32),
+            pltpu.SemaphoreType.DMA((2 + CHUNKS,)),
             pltpu.SemaphoreType.DMA((CHUNKS,)),
         ],
         compiler_params=params(16),
         name="mix",
-    )(kept(back), far(tall), gates, where, weight, target, recency)
+    )(kept(back), far(tall), *[kept(x) for x in (gates, where, weight, target, recency)])
 
 
 def widen_kernel(tall_ref, out_ref):
@@ -395,8 +399,8 @@
         value_target.reshape(1, count), recency.reshape(1, count), experts,
     )
     everyone = exchange(sums.reshape(experts, 1, LANES)).reshape(experts, LANES)
-    total = jnp.sum(everyone, axis=0)
-    return (widen_rows(mixed), values.reshape(count), total[0] / total[1])
+    loss = jnp.sum(everyone[:, 0]) / jnp.sum(everyone[:, 1])
+    return (widen_rows(mixed), values.reshape(count), loss)
 
 
 def solution(mesh):

time: 139 us -> 137 us (0.986)
  Pallas kernels: 25.9 us -> 24.2 us
    unnamed x14 -> x15, local copies, waits for them, and re-layouts: 2.47 us -> 2.98 us
  transfers between devices with their start and end apart: 2 -> 2, of which waited for: 2 -> 2; matrix products, arithmetic and copies ran while one was open for 0% -> 0% of each run, Pallas kernels for 3% -> 4%
where the time goes in v4:
time: 137 us
  blocking collectives  52.7 us (38%)
  waiting for transfers between devices  43 us (31%)
  Pallas kernels  24.2 us (18%)
  starting transfers between devices  9.99 us (7%)
  between operations  3.24 us (2%)
  local copies, waits for them, and re-layouts  2.98 us (2%)
    all_to_all x1, blocking collectives, exchange(): return lax.all_to_all(x, EXPERT, split_axis=0, concat_axis=0, tiled=True)  52.7 us
    all_to_all x2, waiting for transfers between devices, exchange(): return lax.all_to_all(x, EXPERT, split_axis=0, concat_axis=0, tiled=True)  43 us
    pallas_call x1, Pallas kernels, expert_ffn(): pl.pallas_call(ffn_kernel, in_specs=[NEAR] + [FAR] * 3, out_specs=FAR, ou...  12.1 us
    all_to_all x2, starting transfers between devices, exchange(): return lax.all_to_all(x, EXPERT, split_axis=0, concat_axis=0, tiled=True)  9.99 us
    pallas_call x1, Pallas kernels, route(): pl.pallas_call(route_kernel, in_specs=[FAR] * 3, out_specs=FAR, out_shape...  4.16 us
    pallas_call x1, Pallas kernels, mix(): pl.pallas_call(mix_kernel, in_specs=[NEAR, FAR] + [NEAR] * 5, out_specs=[...  3.14 us
    unnamed x15, local copies, waits for them, and re-layouts  2.98 us
  transfers between devices with their start and end apart: 2, of which 2 were waited for; matrix products, arithmetic and copies ran while one was open for 0% of the time, Pallas kernels for 4%

profile of v4, /device:TPU:1, one launch (start us, length us, event | category | flops | bytes accessed | tf_op | source)
XLA Modules:
  0.0 136.9 jit_solution(2425796274700455578)
XLA Ops:
  0.6 4.2 %route.1 = bf16[128,96,128]{2,1,0:T(8,128)(2,1)} custom-call(bf16[128,4096]{1,0:T(8,128)(2,1)} %tok_ref.3, f32[1,4096]{1,0:T(1,128)} %bitcast.18, s32[2,128]{1,0:T(2,128)} %bitcast.20), custom_call_target="tpu_custom_call" | custom-call | tf_op jit(solution)/shard_map/route/pallas_call | solution.py:135
  4.8 52.7 %all_to_all.15 = bf16[128,96,128]{2,1,0:T(8,128)(2,1)S(1)} all-to-all(bf16[128,96,128]{2,1,0:T(8,128)(2,1)} %route.1), channel_id=1, replica_groups=mesh['expert_0'=4,'expert_1'=4,'expert_2'=4,'expert_3'=2] {'expert_0','e..., dimensions={0} | all-to-all | bytes 6291456 | tf_op jit(solution)/shard_map/all_to_all | solution.py:371
  57.5 12.1 %ffn.1 = bf16[384,32,128]{2,1,0:T(8,128)(2,1)} custom-call(bf16[384,32,128]{2,1,0:T(8,128)(2,1)S(1)} %bitcast.17, bf16[1,4096,768]{2,1,0:T(8,128)(2,1)} %gate_ref.1, bf16[1,4096,768]{2,1,0:T(8,128)(2,1)} %up_ref.1, bf16[1,768,4096]{2,1,0:T(8,128)(2,1)} %down_ref.1), custom_call_target="tpu_custom_call" | custom-call | flops 7247757312 | bytes 25165824 | tf_op jit(solution)/shard_map/ffn/pallas_call | solution.py:253
  69.6 0.0 copy-start.6
  69.6 0.0 copy-start.1
  69.6 0.0 copy-start.2
  69.6 5.1 %all-to-all-start.1 = ((bf16[128,96,128]{2,1,0:T(8,128)(2,1)}), bf16[128,96,128]{2,1,0:T(8,128)(2,1)S(1)}, u32[]{:S(2)}, u32[]{:S(2)}) async-start(bf16[128,96,128]{2,1,0:T(8,128)(2,1)} %bitcast.24), calls=%async_computation.1 | async-start | bytes 6291456 | tf_op jit(solution)/shard_map/all_to_all | solution.py:371
  74.7 0.0 copy-done.6
  74.7 0.0 copy-done.1
  74.7 0.0 copy-done.2
  74.7 0.0 copy-start
  74.7 1.2 copy-done
  75.9 0.0 copy-start.5
  75.9 1.2 copy-done.5
  77.2 0.0 copy-start.3
  77.2 0.0 copy-start.4
  77.2 2.2 %gate.1 = (f32[8,128]{1,0:T(8,128)S(1)}, s32[8,128]{1,0:T(8,128)S(1)}, bf16[128,32,128]{2,1,0:T(8,128)(2,1)}) custom-call(bf16[128,4096]{1,0:T(8,128)(2,1)S(1)} %copy-done, f32[1,4096]{1,0:T(1,128)S(1)} %bitcast.19, bf16[4096,128]{1,0:T(8,128)(2,1)S(1)} %copy-done.5, s32[2,128]{1,0:T(2,128)S(1)} %bitcast.21), custom_call_target="tpu_custom_call" | custom-call | flops 10000000000 | bytes 4194304 | tf_op jit(solution)/shard_map/gate/pallas_call | solution.py:187
  79.3 36.7 %all-to-all-done.1 = bf16[128,96,128]{2,1,0:T(8,128)(2,1)S(1)} async-done(((bf16[128,96,128]{2,1,0:T(8,128)(2,1)}), bf16[128,96,128]{2,1,0:T(8,128)(2,1)S(1)}, u32[]{:S(2)}, u32[]{:S(2)}) %all-to-all-start.1) | async-done | bytes 3145760 | tf_op jit(solution)/shard_map/all_to_all | solution.py:371
  116.0 0.0 copy-done.3
  116.0 0.0 copy-done.4
  116.0 3.1 %mix.1 = (bf16[128,32,128]{2,1,0:T(8,128)(2,1)}, f32[1,128]{1,0:T(1,128)S(1)}, f32[128,128]{1,0:T(8,128)}) custom-call(bf16[384,32,128]{2,1,0:T(8,128)(2,1)S(1)} %bitcast.16, bf16[128,32,128]{2,1,0:T(8,128)(2,1)} %get-tuple-element.9.token_ref, f32[8,128]{1,0:T(8,128)S(1)} %get-tuple-element.10.gates_ref, s32[8,128]{1,0:T(8,128)S(1)} %get-tuple-element.11.where_ref, ...), custom_call_target="tpu_custom_call" | custom-call | tf_op jit(solution)/shard_map/mix/pallas_call | solution.py:322
  119.1 4.9 %all-to-all-start.2 = ((f32[128,1,128]{2,1,0:T(1,128)}), f32[128,1,128]{2,1,0:T(1,128)S(1)}, u32[]{:S(2)}, u32[]{:S(2)}) async-start(f32[128,1,128]{2,1,0:T(1,128)} %bitcast.10), calls=%async_computation.2 | async-start | bytes 131072 | tf_op jit(solution)/shard_map/all_to_all | solution.py:371
  124.1 2.7 %widen.1 = bf16[128,4096]{1,0:T(8,128)(2,1)} custom-call(bf16[128,32,128]{2,1,0:T(8,128)(2,1)} %get-tuple-element.12.tall_ref), custom_call_target="tpu_custom_call" | custom-call | flops 10000000000 | bytes 2097152 | tf_op jit(solution)/shard_map/widen/pallas_call | solution.py:359
  126.7 0.5 copy.14
  127.2 6.4 %all-to-all-done.2 = f32[128,1,128]{2,1,0:T(1,128)S(1)} async-done(((f32[128,1,128]{2,1,0:T(1,128)}), f32[128,1,128]{2,1,0:T(1,128)S(1)}, u32[]{:S(2)}, u32[]{:S(2)}) %all-to-all-start.2) | async-done | bytes 65568 | tf_op jit(solution)/shard_map/all_to_all | solution.py:371
  133.6 0.8 slice_reduce_fusion
  (1 shorter events, 0.0 us)
Async XLA Ops:
  69.6 5.1 %copy-start.6 = (bf16[4096]{0:T(1024)(128)(2,1)S(1)}, bf16[4096]{0:T(1024)(128)(2,1)}, u32[]{:S(2)}) copy-start(bf16[4096]{0:T(1024)(128)(2,1)} %param.17) | copy-start | bytes 24580
  69.6 5.1 %copy-start.1 = (f32[4096]{0:T(1024)S(1)}, f32[4096]{0:T(1024)}, u32[]{:S(2)}) copy-start(f32[4096]{0:T(1024)} %param.11) | copy-start | bytes 49156
  69.6 5.1 %copy-start.2 = (s32[128,2]{0,1:T(2,128)S(1)}, s32[128,2]{0,1:T(2,128)}, u32[]{:S(2)}) copy-start(s32[128,2]{0,1:T(2,128)} %param.13) | copy-start | bytes 3076
  69.6 46.4 %all-to-all-start.1 = ((bf16[128,96,128]{2,1,0:T(8,128)(2,1)}), bf16[128,96,128]{2,1,0:T(8,128)(2,1)S(1)}, u32[]{:S(2)}, u32[]{:S(2)}) async-start(bf16[128,96,128]{2,1,0:T(8,128)(2,1)} %bitcast.24), calls=%async_computation.1 | async-start | bytes 6291456 | tf_op jit(solution)/shard_map/all_to_all | solution.py:371
  74.7 1.2 copy-start
  75.9 1.2 copy-start.5
  77.2 38.8 %copy-start.3 = (s32[128]{0:T(128)S(1)}, s32[128]{0:T(128)}, u32[]{:S(2)}) copy-start(s32[128]{0:T(128)} %param.18) | copy-start | bytes 1540
  77.2 38.8 %copy-start.4 = (f32[128]{0:T(128)S(1)}, f32[128]{0:T(128)}, u32[]{:S(2)}) copy-start(f32[128]{0:T(128)} %param.19) | copy-start | bytes 1540
  119.1 14.5 %all-to-all-start.2 = ((f32[128,1,128]{2,1,0:T(1,128)}), f32[128,1,128]{2,1,0:T(1,128)S(1)}, u32[]{:S(2)}, u32[]{:S(2)}) async-start(f32[128,1,128]{2,1,0:T(1,128)} %bitcast.10), calls=%async_computation.2 | async-start | bytes 131072 | tf_op jit(solution)/shard_map/all_to_all | solution.py:371

commit v5 on v4

--- a/solution.py
+++ b/solution.py
@@ -18,6 +18,7 @@
 CHUNKS = 4
 MIB = 1024 * 1024
 NEAR = pl.BlockSpec(memory_space=pltpu.VMEM)
+SCALARS = pl.BlockSpec(memory_space=pltpu.SMEM)
 FAR = pl.BlockSpec(memory_space=pltpu.HBM)
 
 
@@ -154,20 +155,27 @@
     )(far(tokens), far(norm_gain), far(ids))
 
 
-def gate_kernel(tok_ref, gain_ref, router_ref, ids_ref, gates_ref, where_ref, tall_ref, normed_ref):
+def gate_kernel(
+    *refs,
+):
+    inputs, (gates_ref, where_ref, base_ref), scratch = refs[:5], refs[5:8], refs[8:]
+    tok_ref, gain_ref, router_ref, ids_ref, weight_ref, normed_ref, score_ref, sems = scratch
+    for copy in start_all(zip(inputs, scratch[:5]), sems):
+        copy.wait()
     count, width = tok_ref.shape
-    parts = width // LANES
     experts = router_ref.shape[1]
     gain = gain_ref[...]
+    weight = weight_ref[...]
 
     def norm_rows(step, carry):
         start = pl.multiple_of(step * ROWS, ROWS)
         wide = tok_ref[pl.ds(start, ROWS), :].astype(F32)
         normed_ref[pl.ds(start, ROWS), :] = norm(wide, gain)
-        tall_ref[pl.ds(start, ROWS)] = wide.reshape(ROWS, parts, LANES).astype(BF16)
+        score_ref[pl.ds(start, ROWS), :] = jnp.sum(wide * weight, axis=1, keepdims=True)
         return carry
 
     lax.fori_loop(0, count // ROWS, norm_rows, 0)
+    base_ref[...] = to_row(score_ref[...])
     hits, rank = slots_of(ids_ref, experts)
     logits = jnp.transpose(jnp.dot(normed_ref[...], router_ref[...], preferred_element_type=F32))
     scores = []
@@ -181,39 +189,42 @@
     gates_ref[1:2, :] = jax.nn.sigmoid(scores[1] - scores[0])
 
 
-def gate(tokens, norm_gain, router_weight, ids):
+def gate(tokens, norm_gain, router_weight, ids, weight):
     count, width = tokens.shape
-    parts = width // LANES
+    inputs = (tokens, norm_gain, router_weight, ids, weight)
     return pl.pallas_call(
         gate_kernel,
-        in_specs=[NEAR] * 4,
+        in_specs=[FAR] * 5,
         out_specs=[NEAR] * 3,
         out_shape=[
             jax.ShapeDtypeStruct((8, count), F32),
             jax.ShapeDtypeStruct((8, count), I32),
-            pltpu.HBM((count, parts, LANES), BF16),
+            jax.ShapeDtypeStruct((1, count), F32),
         ],
-        scratch_shapes=[pltpu.VMEM((count, width), BF16)],
+        scratch_shapes=[pltpu.VMEM(x.shape, x.dtype) for x in inputs]
+        + [pltpu.VMEM((count, width), BF16), pltpu.VMEM((count, 1), F32), pltpu.SemaphoreType.DMA((5,))],
         compiler_params=params(16),
         cost_estimate=cost(10**10, 4 * MIB),
         name="gate",
-    )(tokens, norm_gain, router_weight, ids)
+    )(*[far(x) for x in inputs])
 
 
 def ffn_kernel(
     in_ref, gate_ref, up_ref, down_ref, out_ref,
-    gate_near, up_near, down_near, wide_ref, hidden_ref, tall_ref, sems, out_sems,
+    both_near, down_near, wide_ref, hidden_ref, tall_ref, part_ref, sems, out_sems,
 ):
     rows, parts, _ = in_ref.shape
-    width, hidden = gate_near.shape
-    tiles = [slice(start, start + 256) for start in range(0, hidden, 256)]
+    hidden, width = down_near.shape
+    half = width // 2
+    tile = both_near.shape[2] // 2
+    blocks = [(0, slice(0, half)), (0, slice(half, width))]
+    blocks += [(i, slice(0, width)) for i in range(1, hidden // tile)]
     pairs = []
-    for tile in tiles:
-        pairs.append((gate_ref.at[0, :, tile], gate_near.at[:, tile]))
-        pairs.append((up_ref.at[0, :, tile], up_near.at[:, tile]))
-    for tile in tiles:
-        pairs.append((down_ref.at[0, tile, :], down_near.at[tile, :]))
-    copies = start_all(pairs, sems)
+    for i, deep in blocks:
+        columns = slice(i * tile, (i + 1) * tile)
+        pairs.append((gate_ref.at[0, deep, columns], both_near.at[i, deep, 0:tile]))
+        pairs.append((up_ref.at[0, deep, columns], both_near.at[i, deep, tile:2 * tile]))
+    copies = start_all(pairs + [(down_ref.at[0], down_near)], sems)
 
     def widen(i, carry):
         start = pl.multiple_of(i * ROWS, ROWS)
@@ -222,16 +233,17 @@
         return carry
 
     lax.fori_loop(0, rows // ROWS, widen, 0)
-    for i, tile in enumerate(tiles):
-        copies[2 * i].wait()
-        copies[2 * i + 1].wait()
-        x = wide_ref[...]
-        gated = jnp.dot(x, gate_near[:, tile], preferred_element_type=F32)
-        upped = jnp.dot(x, up_near[:, tile], preferred_element_type=F32)
-        hidden_ref[:, tile] = (jax.nn.silu(gated) * upped).astype(BF16)
-    for i in range(len(tiles)):
-        copies[2 * len(tiles) + i].wait()
-    half = width // 2
+    for n, (i, deep) in enumerate(blocks):
+        copies[2 * n].wait()
+        copies[2 * n + 1].wait()
+        both = jnp.dot(wide_ref[:, deep], both_near[i, deep, :], preferred_element_type=F32)
+        if n == 0:
+            part_ref[...] = both
+            continue
+        if n == 1:
+            both = both + part_ref[...]
+        hidden_ref[:, i * tile:(i + 1) * tile] = (jax.nn.silu(both[:, :tile]) * both[:, tile:]).astype(BF16)
+    copies[-1].wait()
     sent = []
     for p, start in enumerate(range(0, rows, BLOCK)):
         piece = slice(start, start + BLOCK)
@@ -250,62 +262,49 @@
 def expert_ffn(received, gate_proj, up_proj, down_proj):
     rows, parts, _ = received.shape
     _, width, hidden = gate_proj.shape
+    tile = 256
     return pl.pallas_call(
         ffn_kernel,
         in_specs=[NEAR] + [FAR] * 3,
         out_specs=FAR,
         out_shape=pltpu.HBM(received.shape, BF16),
         scratch_shapes=[
-            pltpu.VMEM((width, hidden), BF16),
-            pltpu.VMEM((width, hidden), BF16),
+            pltpu.VMEM((hidden // tile, width, 2 * tile), BF16),
             pltpu.VMEM((hidden, width), BF16),
             pltpu.VMEM((rows, width), BF16),
             pltpu.VMEM((rows, hidden), BF16),
             pltpu.VMEM((rows, parts, LANES), BF16),
-            pltpu.SemaphoreType.DMA((3 * (hidden // 256),)),
+            pltpu.VMEM((rows, 2 * tile), F32),
+            pltpu.SemaphoreType.DMA((2 * (hidden // tile) + 3,)),
             pltpu.SemaphoreType.DMA((rows // BLOCK,)),
         ],
-        compiler_params=params(44),
+        compiler_params=params(48),
         cost_estimate=cost(6 * rows * width * hidden, 24 * MIB),
         name="ffn",
     )(kept(received), far(gate_proj), far(up_proj), far(down_proj))
 
 
-def mix_kernel(
-    back_ref, token_ref, gates_ref, where_ref, weight_ref, target_ref, recency_ref,
-    mixed_ref, values_ref, sums_ref,
-    tall_ref, near_ref, score_ref, gates_smem, where_smem, sems, out_sems,
-):
-    count, parts, _ = token_ref.shape
-    rows = pieces_of(count, CHUNKS)
-    copies = start_all(
-        [(gates_ref, gates_smem), (where_ref, where_smem)] + [(token_ref.at[r], tall_ref.at[r]) for r in rows], sems
-    )
+def value_kernel(
+    back_ref, gates_ref, where_ref, base_ref, weight_ref, target_ref, recency_ref,
+    values_ref, sums_ref, score_ref, gates_smem, where_smem, sems,
+):
+    count = base_ref.shape[1]
+    parts = weight_ref.shape[0]
+    for copy in start_all([(gates_ref, gates_smem), (where_ref, where_smem)], sems):
+        copy.wait()
     weight = weight_ref[...]
-    chunk = count // CHUNKS
-    sent = []
-    copies[0].wait()
-    copies[1].wait()
-    for c in range(CHUNKS):
-        copies[2 + c].wait()
-
-        def mix_rows(step, carry, c=c):
-            for i in range(16):
-                t = c * chunk + step * 16 + i
-                total = tall_ref[t].astype(F32)
-                for k in range(2):
-                    total = total + gates_smem[k, t] * back_ref[where_smem[k, t]].astype(F32)
-                mixed = total.astype(BF16)
-                near_ref[t] = mixed
-                scored = mixed.astype(F32) * weight
-                score_ref[t] = jnp.sum(scored.reshape(parts // 8, 8, LANES), axis=0)
-            return carry
-
-        lax.fori_loop(0, chunk // 16, mix_rows, 0)
-        sent.append(pltpu.make_async_copy(near_ref.at[rows[c]], mixed_ref.at[rows[c]], out_sems.at[c]))
-        sent[c].start()
+
+    def score_rows(step, carry):
+        for i in range(16):
+            t = step * 16 + i
+            first = gates_smem[0, t] * back_ref[where_smem[0, t]].astype(F32)
+            mixed = first + gates_smem[1, t] * back_ref[where_smem[1, t]].astype(F32)
+            score_ref[t] = jnp.sum((mixed * weight).reshape(parts // 8, 8, LANES), axis=0)
+        return carry
+
+    lax.fori_loop(0, count // 16, score_rows, 0)
     by_lane = jnp.sum(score_ref[...], axis=1)
-    values = jnp.tanh(to_row(jnp.sum(by_lane, axis=1, keepdims=True)))
+    values = jnp.tanh(base_ref[...] + to_row(jnp.sum(by_lane, axis=1, keepdims=True)))
     values_ref[...] = values
     error = values - target_ref[...].astype(F32)
     recency = recency_ref[...]
@@ -313,58 +312,74 @@
     total = jnp.sum(recency, axis=1, keepdims=True)
     lane = iota(sums_ref.shape, 1)
     sums_ref[...] = jnp.where(lane == 0, weighted, jnp.where(lane == 1, total, 0.0))
-    for copy in sent:
-        copy.wait()
-
-
-def mix(back, tall, gates, where, weight, target, recency, devices):
-    count, parts, _ = tall.shape
+
+
+def value(back, gates, where, base, weight, target, recency, devices):
+    count = base.shape[1]
     return pl.pallas_call(
-        mix_kernel,
-        in_specs=[NEAR, FAR] + [NEAR] * 5,
-        out_specs=[FAR] + [NEAR] * 2,
-        out_shape=[
-            pltpu.HBM(tall.shape, BF16),
-            pltpu.VMEM((1, count), F32),
-            pltpu.VMEM((devices, LANES), F32),
-        ],
+        value_kernel,
+        in_specs=[NEAR] * 7,
+        out_specs=[NEAR] * 2,
+        out_shape=[pltpu.VMEM(base.shape, F32), pltpu.VMEM((devices, LANES), F32)],
         scratch_shapes=[
-            pltpu.VMEM((count, parts, LANES), BF16),
-            pltpu.VMEM((count, parts, LANES), BF16),
             pltpu.VMEM((count, 8, LANES), F32),
             pltpu.SMEM(gates.shape, F32),
             pltpu.SMEM(where.shape, I32),
-            pltpu.SemaphoreType.DMA((2 + CHUNKS,)),
+            pltpu.SemaphoreType.DMA((2,)),
+        ],
+        compiler_params=params(8),
+        name="value",
+    )(*[kept(x) for x in (back, gates, where, base, weight, target, recency)])
+
+
+def mix_kernel(
+    back_ref, token_ref, gates_ref, where_ref, mixed_ref, near_ref, out_near, sum_ref, sems, out_sems
+):
+    count, width = token_ref.shape
+    parts = width // LANES
+    rows = pieces_of(count, CHUNKS)
+    copies = start_all([(token_ref.at[r], near_ref.at[r]) for r in rows], sems)
+    chunk = count // CHUNKS
+    sent = []
+    for c in range(CHUNKS):
+        copies[c].wait()
+
+        def mix_rows(step, carry, c=c):
+            start = pl.multiple_of(c * chunk + step * ROWS, ROWS)
+            for i in range(ROWS):
+                t = start + i
+                first = gates_ref[0, t] * back_ref[where_ref[0, t]].astype(F32)
+                sum_ref[i] = first + gates_ref[1, t] * back_ref[where_ref[1, t]].astype(F32)
+            update = sum_ref[...].reshape(ROWS, width)
+            mixed = near_ref[pl.ds(start, ROWS), :].astype(F32) + update
+            out_near[pl.ds(start, ROWS), :] = mixed.astype(BF16)
+            return carry
+
+        lax.fori_loop(0, chunk // ROWS, mix_rows, 0)
+        sent.append(pltpu.make_async_copy(out_near.at[rows[c]], mixed_ref.at[rows[c]], out_sems.at[c]))
+        sent[c].start()
+    for copy in sent:
+        copy.wait()
+
+
+def mix(back, tokens, gates, where):
+    count, width = tokens.shape
+    return pl.pallas_call(
+        mix_kernel,
+        in_specs=[NEAR, FAR] + [SCALARS] * 2,
+        out_specs=FAR,
+        out_shape=pltpu.HBM(tokens.shape, BF16),
+        scratch_shapes=[
+            pltpu.VMEM(tokens.shape, BF16),
+            pltpu.VMEM(tokens.shape, BF16),
+            pltpu.VMEM((ROWS, width // LANES, LANES), F32),
+            pltpu.SemaphoreType.DMA((CHUNKS,)),
             pltpu.SemaphoreType.DMA((CHUNKS,)),
         ],
         compiler_params=params(16),
+        cost_estimate=cost(10**10, 6 * MIB),
         name="mix",
-    )(kept(back), far(tall), *[kept(x) for x in (gates, where, weight, target, recency)])
-
-
-def widen_kernel(tall_ref, out_ref):
-    count, width = out_ref.shape
-
-    def widen(i, carry):
-        start = pl.multiple_of(i * ROWS, ROWS)
-        tall = tall_ref[pl.ds(start, ROWS)].astype(F32)
-        out_ref[pl.ds(start, ROWS), :] = tall.reshape(ROWS, width).astype(BF16)
-        return carry
-
-    lax.fori_loop(0, count // ROWS, widen, 0)
-
-
-def widen_rows(tall):
-    count, parts, _ = tall.shape
-    return pl.pallas_call(
-        widen_kernel,
-        in_specs=[NEAR],
-        out_specs=NEAR,
-        out_shape=jax.ShapeDtypeStruct((count, parts * LANES), BF16),
-        compiler_params=params(8),
-        cost_estimate=cost(10**10, 2 * MIB),
-        name="widen",
-    )(far(tall))
+    )(kept(back), far(tokens), gates, where)
 
 
 def exchange(x):
@@ -391,16 +406,17 @@
     ids = expert_ids.T
     gain = norm_gain.reshape(1, width)
     received = exchange(route(tokens, gain, ids, experts))
-    gates, where, tall = gate(tokens, gain, router_weight, ids)
+    weight = value_weight.astype(F32)
+    gates, where, base = gate(tokens, gain, router_weight, ids, weight.reshape(1, width))
     produced = expert_ffn(received.reshape(rows), gate_proj, up_proj, down_proj)
-    back = exchange(produced.reshape(pieces))
-    mixed, values, sums = mix(
-        back.reshape(rows), tall, gates, where, value_weight.reshape(parts, LANES).astype(F32),
+    back = exchange(produced.reshape(pieces)).reshape(rows)
+    values, sums = value(
+        back, gates, where, base, weight.reshape(parts, LANES),
         value_target.reshape(1, count), recency.reshape(1, count), experts,
     )
     everyone = exchange(sums.reshape(experts, 1, LANES)).reshape(experts, LANES)
-    loss = jnp.sum(everyone[:, 0]) / jnp.sum(everyone[:, 1])
-    return (widen_rows(mixed), values.reshape(count), loss)
+    mixed = mix(back, tokens, gates, where)
+    return (mixed, values.reshape(count), jnp.sum(everyone[:, 0]) / jnp.sum(everyone[:, 1]))
 
 
 def solution(mesh):

time: 137 us -> 136 us (level)
  local copies, waits for them, and re-layouts: 2.98 us -> 0.53 us
    unnamed x15 -> x7, local copies, waits for them, and re-layouts: 2.98 us -> 0.53 us
  transfers between devices with their start and end apart: 2 -> 2, of which waited for: 2 -> 2; matrix products, arithmetic and copies ran while one was open for 0% -> 1% of each run, Pallas kernels for 4% -> 5%
where the time goes in v5:
time: 136 us; the launch traced here: 135 us
  blocking collectives  52.7 us (39%)
  waiting for transfers between devices  42.9 us (32%)
  Pallas kernels  24.8 us (18%)
  starting transfers between devices  9.96 us (7%)
  between operations  3.08 us (2%)
    all_to_all x1, blocking collectives, exchange(): return lax.all_to_all(x, EXPERT, split_axis=0, concat_axis=0, tiled=True)  52.7 us
    all_to_all x2, waiting for transfers between devices, exchange(): return lax.all_to_all(x, EXPERT, split_axis=0, concat_axis=0, tiled=True)  42.9 us
    pallas_call x1, Pallas kernels, expert_ffn(): pl.pallas_call(ffn_kernel, in_specs=[NEAR] + [FAR] * 3, out_specs=FAR, ou...  11.6 us
    all_to_all x2, starting transfers between devices, exchange(): return lax.all_to_all(x, EXPERT, split_axis=0, concat_axis=0, tiled=True)  9.96 us
    pallas_call x1, Pallas kernels, route(): pl.pallas_call(route_kernel, in_specs=[FAR] * 3, out_specs=FAR, out_shape...  4.18 us
    pallas_call x1, Pallas kernels, mix(): pl.pallas_call(mix_kernel, in_specs=[NEAR, FAR] + [SCALARS] * 2, out_spec...  3.49 us
    pallas_call x1, Pallas kernels, gate(): pl.pallas_call(gate_kernel, in_specs=[FAR] * 5, out_specs=[NEAR] * 3, out...  3.36 us
  transfers between devices with their start and end apart: 2, of which 2 were waited for; matrix products, arithmetic and copies ran while one was open for 1% of the time, Pallas kernels for 5%

profile of v5, /device:TPU:1, one launch (start us, length us, event | category | flops | bytes accessed | tf_op | source)
XLA Modules:
  0.0 135.2 jit_solution(8924028513003688276)
XLA Ops:
  0.6 4.2 %route.1 = bf16[128,96,128]{2,1,0:T(8,128)(2,1)} custom-call(bf16[128,4096]{1,0:T(8,128)(2,1)} %token_ref.1, f32[1,4096]{1,0:T(1,128)} %bitcast.23, s32[2,128]{1,0:T(2,128)} %bitcast.26), custom_call_target="tpu_custom_call" | custom-call | tf_op jit(solution)/shard_map/route/pallas_call | solution.py:136
  4.8 52.7 %all_to_all.15 = bf16[128,96,128]{2,1,0:T(8,128)(2,1)S(1)} all-to-all(bf16[128,96,128]{2,1,0:T(8,128)(2,1)} %route.1), channel_id=1, replica_groups=mesh['expert_0'=4,'expert_1'=4,'expert_2'=4,'expert_3'=2] {'expert_0','e..., dimensions={0} | all-to-all | bytes 6291456 | tf_op jit(solution)/shard_map/all_to_all | solution.py:386
  57.5 11.6 %ffn.1 = bf16[384,32,128]{2,1,0:T(8,128)(2,1)} custom-call(bf16[384,32,128]{2,1,0:T(8,128)(2,1)S(1)} %bitcast.18, bf16[1,4096,768]{2,1,0:T(8,128)(2,1)} %gate_ref.1, bf16[1,4096,768]{2,1,0:T(8,128)(2,1)} %up_ref.1, bf16[1,768,4096]{2,1,0:T(8,128)(2,1)} %down_ref.1), custom_call_target="tpu_custom_call" | custom-call | flops 7247757312 | bytes 25165824 | tf_op jit(solution)/shard_map/ffn/pallas_call | solution.py:266
  69.1 0.0 copy-start.2
  69.1 5.0 %all-to-all-start.1 = ((bf16[128,96,128]{2,1,0:T(8,128)(2,1)}), bf16[128,96,128]{2,1,0:T(8,128)(2,1)S(1)}, u32[]{:S(2)}, u32[]{:S(2)}) async-start(bf16[128,96,128]{2,1,0:T(8,128)(2,1)} %bitcast.21), calls=%async_computation.1 | async-start | bytes 6291456 | tf_op jit(solution)/shard_map/all_to_all | solution.py:386
  74.2 0.0 copy-done.2
  74.2 0.6 convert_bitcast_fusion
  74.8 0.0 copy-start
  74.8 0.0 copy-start.1
  74.8 3.4 %gate.1 = (f32[8,128]{1,0:T(8,128)S(1)}, s32[8,128]{1,0:T(8,128)S(1)}, f32[1,128]{1,0:T(1,128)S(1)}) custom-call(bf16[128,4096]{1,0:T(8,128)(2,1)} %token_ref.1, f32[1,4096]{1,0:T(1,128)} %bitcast.24, bf16[4096,128]{1,0:T(8,128)(2,1)} %refs_2_.1, s32[2,128]{1,0:T(2,128)} %bitcast.27, f32[1,4096]{1,0:T(1,128)} %bitcast.25), custom_call_target="tpu_custom_call" | custom-call | flops 10000000000 | bytes 4194304 | tf_op jit(solution)/shard_map/gate/pallas_call | solution.py:195
  78.2 37.3 %all-to-all-done.1 = bf16[128,96,128]{2,1,0:T(8,128)(2,1)S(1)} async-done(((bf16[128,96,128]{2,1,0:T(8,128)(2,1)}), bf16[128,96,128]{2,1,0:T(8,128)(2,1)S(1)}, u32[]{:S(2)}, u32[]{:S(2)}) %all-to-all-start.1) | async-done | bytes 3145760 | tf_op jit(solution)/shard_map/all_to_all | solution.py:386
  115.5 0.0 copy-done
  115.5 0.0 copy-done.1
  115.5 2.2 %value.1 = (f32[1,128]{1,0:T(1,128)S(1)}, f32[128,128]{1,0:T(8,128)}) custom-call(bf16[384,32,128]{2,1,0:T(8,128)(2,1)S(1)} %bitcast.16, f32[8,128]{1,0:T(8,128)S(1)} %get-tuple-element.8.gates_ref, s32[8,128]{1,0:T(8,128)S(1)} %get-tuple-element.9.where_ref, f32[1,128]{1,0:T(1,128)S(1)} %get-tuple-element.10.base_ref, ...), custom_call_target="tpu_custom_call" | custom-call | tf_op jit(solution)/shard_map/value/pallas_call | solution.py:319
  117.7 4.9 %all-to-all-start.2 = ((f32[128,1,128]{2,1,0:T(1,128)}), f32[128,1,128]{2,1,0:T(1,128)S(1)}, u32[]{:S(2)}, u32[]{:S(2)}) async-start(f32[128,1,128]{2,1,0:T(1,128)} %bitcast.11), calls=%async_computation.2 | async-start | bytes 131072 | tf_op jit(solution)/shard_map/all_to_all | solution.py:386
  122.6 3.5 %mix.1 = bf16[128,4096]{1,0:T(8,128)(2,1)} custom-call(bf16[384,32,128]{2,1,0:T(8,128)(2,1)S(1)} %bitcast.17, bf16[128,4096]{1,0:T(8,128)(2,1)} %token_ref.1, f32[8,128]{1,0:T(8,128)S(1)} %get-tuple-element.8.gates_ref, s32[8,128]{1,0:T(8,128)S(1)} %get-tuple-element.9.where_ref), custom_call_target="tpu_custom_call" | custom-call | flops 10000000000 | bytes 6291456 | tf_op jit(solution)/shard_map/mix/pallas_call | solution.py:367
  126.1 0.5 copy.14
  126.6 5.6 %all-to-all-done.2 = f32[128,1,128]{2,1,0:T(1,128)S(1)} async-done(((f32[128,1,128]{2,1,0:T(1,128)}), f32[128,1,128]{2,1,0:T(1,128)S(1)}, u32[]{:S(2)}, u32[]{:S(2)}) %all-to-all-start.2) | async-done | bytes 65568 | tf_op jit(solution)/shard_map/all_to_all | solution.py:386
  132.1 0.7 slice_reduce_fusion
Async XLA Ops:
  69.1 5.1 %copy-start.2 = (bf16[4096]{0:T(1024)(128)(2,1)S(1)}, bf16[4096]{0:T(1024)(128)(2,1)}, u32[]{:S(2)}) copy-start(bf16[4096]{0:T(1024)(128)(2,1)} %param.17) | copy-start | bytes 24580
  69.1 46.4 %all-to-all-start.1 = ((bf16[128,96,128]{2,1,0:T(8,128)(2,1)}), bf16[128,96,128]{2,1,0:T(8,128)(2,1)S(1)}, u32[]{:S(2)}, u32[]{:S(2)}) async-start(bf16[128,96,128]{2,1,0:T(8,128)(2,1)} %bitcast.21), calls=%async_computation.1 | async-start | bytes 6291456 | tf_op jit(solution)/shard_map/all_to_all | solution.py:386
  74.8 40.7 %copy-start = (s32[128]{0:T(128)S(1)}, s32[128]{0:T(128)}, u32[]{:S(2)}) copy-start(s32[128]{0:T(128)} %param.18) | copy-start | bytes 1540
  74.8 40.7 %copy-start.1 = (f32[128]{0:T(128)S(1)}, f32[128]{0:T(128)}, u32[]{:S(2)}) copy-start(f32[128]{0:T(128)} %param.19) | copy-start | bytes 1540
  117.7 14.5 %all-to-all-start.2 = ((f32[128,1,128]{2,1,0:T(1,128)}), f32[128,1,128]{2,1,0:T(1,128)S(1)}, u32[]{:S(2)}, u32[]{:S(2)}) async-start(f32[128,1,128]{2,1,0:T(1,128)} %bitcast.11), calls=%async_computation.2 | async-start | bytes 131072 | tf_op jit(solution)/shard_map/all_to_all | solution.py:386

commit v6 on v5

--- a/solution.py
+++ b/solution.py
@@ -158,8 +158,8 @@
 def gate_kernel(
     *refs,
 ):
-    inputs, (gates_ref, where_ref, base_ref), scratch = refs[:5], refs[5:8], refs[8:]
-    tok_ref, gain_ref, router_ref, ids_ref, weight_ref, normed_ref, score_ref, sems = scratch
+    inputs, (gates_out, where_out, base_ref), scratch = refs[:5], refs[5:8], refs[8:]
+    tok_ref, gain_ref, router_ref, ids_ref, weight_ref, normed_ref, score_ref, gates_ref, where_ref, sems = scratch
     for copy in start_all(zip(inputs, scratch[:5]), sems):
         copy.wait()
     count, width = tok_ref.shape
@@ -187,6 +187,8 @@
         scores.append(jnp.sum(jnp.where(hits[k], logits, 0.0), axis=0, keepdims=True))
     gates_ref[0:1, :] = jax.nn.sigmoid(scores[0] - scores[1])
     gates_ref[1:2, :] = jax.nn.sigmoid(scores[1] - scores[0])
+    for copy in start_all([(gates_ref, gates_out), (where_ref, where_out)], sems):
+        copy.wait()
 
 
 def gate(tokens, norm_gain, router_weight, ids, weight):
@@ -195,14 +197,15 @@
     return pl.pallas_call(
         gate_kernel,
         in_specs=[FAR] * 5,
-        out_specs=[NEAR] * 3,
+        out_specs=[SCALARS, SCALARS, NEAR],
         out_shape=[
-            jax.ShapeDtypeStruct((8, count), F32),
-            jax.ShapeDtypeStruct((8, count), I32),
+            pltpu.SMEM((8, count), F32),
+            pltpu.SMEM((8, count), I32),
             jax.ShapeDtypeStruct((1, count), F32),
         ],
         scratch_shapes=[pltpu.VMEM(x.shape, x.dtype) for x in inputs]
-        + [pltpu.VMEM((count, width), BF16), pltpu.VMEM((count, 1), F32), pltpu.SemaphoreType.DMA((5,))],
+        + [pltpu.VMEM((count, width), BF16), pltpu.VMEM((count, 1), F32)]
+        + [pltpu.VMEM((8, count), F32), pltpu.VMEM((8, count), I32), pltpu.SemaphoreType.DMA((5,))],
         compiler_params=params(16),
         cost_estimate=cost(10**10, 4 * MIB),
         name="gate",
@@ -233,16 +236,22 @@
         return carry
 
     lax.fori_loop(0, rows // ROWS, widen, 0)
+
+    def join(i):
+        both = part_ref.at[i % 2]
+        hidden_ref[:, i * tile:(i + 1) * tile] = (jax.nn.silu(both[:, :tile]) * both[:, tile:]).astype(BF16)
+
     for n, (i, deep) in enumerate(blocks):
         copies[2 * n].wait()
         copies[2 * n + 1].wait()
         both = jnp.dot(wide_ref[:, deep], both_near[i, deep, :], preferred_element_type=F32)
-        if n == 0:
-            part_ref[...] = both
+        if n == 1:
+            part_ref[0] += both
             continue
-        if n == 1:
-            both = both + part_ref[...]
-        hidden_ref[:, i * tile:(i + 1) * tile] = (jax.nn.silu(both[:, :tile]) * both[:, tile:]).astype(BF16)
+        part_ref[i % 2] = both
+        if i > 0:
+            join(i - 1)
+    join(hidden // tile - 1)
     copies[-1].wait()
     sent = []
     for p, start in enumerate(range(0, rows, BLOCK)):
@@ -252,9 +261,10 @@
                 hidden_ref[piece, :], down_near[:, side * half:(side + 1) * half], preferred_element_type=F32
             )
             tall = wide.reshape(BLOCK, parts // 2, LANES).astype(BF16)
-            tall_ref[piece, side * (parts // 2):(side + 1) * (parts // 2)] = tall
-        sent.append(pltpu.make_async_copy(tall_ref.at[piece], out_ref.at[piece], out_sems.at[p]))
-        sent[p].start()
+            at = (piece, slice(side * (parts // 2), (side + 1) * (parts // 2)))
+            tall_ref[at] = tall
+            sent.append(pltpu.make_async_copy(tall_ref.at[at], out_ref.at[at], out_sems.at[2 * p + side]))
+            sent[-1].start()
     for copy in sent:
         copy.wait()
 
@@ -274,9 +284,9 @@
             pltpu.VMEM((rows, width), BF16),
             pltpu.VMEM((rows, hidden), BF16),
             pltpu.VMEM((rows, parts, LANES), BF16),
-            pltpu.VMEM((rows, 2 * tile), F32),
+            pltpu.VMEM((2, rows, 2 * tile), F32),
             pltpu.SemaphoreType.DMA((2 * (hidden // tile) + 3,)),
-            pltpu.SemaphoreType.DMA((rows // BLOCK,)),
+            pltpu.SemaphoreType.DMA((2 * (rows // BLOCK),)),
         ],
         compiler_params=params(48),
         cost_estimate=cost(6 * rows * width * hidden, 24 * MIB),
@@ -285,13 +295,11 @@
 
 
 def value_kernel(
-    back_ref, gates_ref, where_ref, base_ref, weight_ref, target_ref, recency_ref,
-    values_ref, sums_ref, score_ref, gates_smem, where_smem, sems,
+    back_ref, gates_smem, where_smem, base_ref, weight_ref, target_ref, recency_ref,
+    values_ref, sums_ref, score_ref,
 ):
     count = base_ref.shape[1]
     parts = weight_ref.shape[0]
-    for copy in start_all([(gates_ref, gates_smem), (where_ref, where_smem)], sems):
-        copy.wait()
     weight = weight_ref[...]
 
     def score_rows(step, carry):
@@ -318,18 +326,13 @@
     count = base.shape[1]
     return pl.pallas_call(
         value_kernel,
-        in_specs=[NEAR] * 7,
+        in_specs=[NEAR, SCALARS, SCALARS] + [NEAR] * 4,
         out_specs=[NEAR] * 2,
         out_shape=[pltpu.VMEM(base.shape, F32), pltpu.VMEM((devices, LANES), F32)],
-        scratch_shapes=[
-            pltpu.VMEM((count, 8, LANES), F32),
-            pltpu.SMEM(gates.shape, F32),
-            pltpu.SMEM(where.shape, I32),
-            pltpu.SemaphoreType.DMA((2,)),
-        ],
+        scratch_shapes=[pltpu.VMEM((count, 8, LANES), F32)],
         compiler_params=params(8),
         name="value",
-    )(*[kept(x) for x in (back, gates, where, base, weight, target, recency)])
+    )(kept(back), gates, where, *[kept(x) for x in (base, weight, target, recency)])
 
 
 def mix_kernel(

time: 136 us -> 135 us (level)
  no operation moved by 1% of the time
where the time goes in v6:
time: 135 us; the launch traced here: 134 us
  blocking collectives  52.7 us (39%)
  waiting for transfers between devices  42.9 us (32%)
  Pallas kernels  24 us (18%)
  starting transfers between devices  9.95 us (7%)
  between operations  3.07 us (2%)
    all_to_all x1, blocking collectives, exchange(): return lax.all_to_all(x, EXPERT, split_axis=0, concat_axis=0, tiled=True)  52.7 us
    all_to_all x2, waiting for transfers between devices, exchange(): return lax.all_to_all(x, EXPERT, split_axis=0, concat_axis=0, tiled=True)  42.9 us
    pallas_call x1, Pallas kernels, expert_ffn(): pl.pallas_call(ffn_kernel, in_specs=[NEAR] + [FAR] * 3, out_specs=FAR, ou...  11.5 us
    all_to_all x2, starting transfers between devices, exchange(): return lax.all_to_all(x, EXPERT, split_axis=0, concat_axis=0, tiled=True)  9.95 us
    pallas_call x1, Pallas kernels, route(): pl.pallas_call(route_kernel, in_specs=[FAR] * 3, out_specs=FAR, out_shape...  4.18 us
    pallas_call x1, Pallas kernels, gate(): pl.pallas_call(gate_kernel, in_specs=[FAR] * 5, out_specs=[SCALARS, SCALA...  4.02 us
    pallas_call x1, Pallas kernels, mix(): pl.pallas_call(mix_kernel, in_specs=[NEAR, FAR] + [SCALARS] * 2, out_spec...  2.83 us
  transfers between devices with their start and end apart: 2, of which 2 were waited for; matrix products, arithmetic and copies ran while one was open for 1% of the time, Pallas kernels for 5%

profile of v6, /device:TPU:1, one launch (start us, length us, event | category | flops | bytes accessed | tf_op | source)
XLA Modules:
  0.0 134.4 jit_solution(3003123149611543922)
XLA Ops:
  0.6 4.2 %route.1 = bf16[128,96,128]{2,1,0:T(8,128)(2,1)} custom-call(bf16[128,4096]{1,0:T(8,128)(2,1)} %token_ref.1, f32[1,4096]{1,0:T(1,128)} %bitcast.23, s32[2,128]{1,0:T(2,128)} %bitcast.26), custom_call_target="tpu_custom_call" | custom-call | tf_op jit(solution)/shard_map/route/pallas_call | solution.py:136
  4.8 52.7 %all_to_all.15 = bf16[128,96,128]{2,1,0:T(8,128)(2,1)S(1)} all-to-all(bf16[128,96,128]{2,1,0:T(8,128)(2,1)} %route.1), channel_id=1, replica_groups=mesh['expert_0'=4,'expert_1'=4,'expert_2'=4,'expert_3'=2] {'expert_0','e..., dimensions={0} | all-to-all | bytes 6291456 | tf_op jit(solution)/shard_map/all_to_all | solution.py:389
  57.5 11.5 %ffn.1 = bf16[384,32,128]{2,1,0:T(8,128)(2,1)} custom-call(bf16[384,32,128]{2,1,0:T(8,128)(2,1)S(1)} %bitcast.18, bf16[1,4096,768]{2,1,0:T(8,128)(2,1)} %gate_ref.1, bf16[1,4096,768]{2,1,0:T(8,128)(2,1)} %up_ref.1, bf16[1,768,4096]{2,1,0:T(8,128)(2,1)} %down_ref.1), custom_call_target="tpu_custom_call" | custom-call | flops 7247757312 | bytes 25165824 | tf_op jit(solution)/shard_map/ffn/pallas_call | solution.py:276
  69.0 0.0 copy-start.2
  69.0 5.1 %all-to-all-start.1 = ((bf16[128,96,128]{2,1,0:T(8,128)(2,1)}), bf16[128,96,128]{2,1,0:T(8,128)(2,1)S(1)}, u32[]{:S(2)}, u32[]{:S(2)}) async-start(bf16[128,96,128]{2,1,0:T(8,128)(2,1)} %bitcast.21), calls=%async_computation.1 | async-start | bytes 6291456 | tf_op jit(solution)/shard_map/all_to_all | solution.py:389
  74.1 0.0 copy-done.2
  74.1 0.6 convert_bitcast_fusion
  74.7 0.0 copy-start
  74.7 0.0 copy-start.1
  74.7 4.0 %gate.1 = (f32[8,128]{1,0:T(8,128)S(4)}, s32[8,128]{1,0:T(8,128)S(4)}, f32[1,128]{1,0:T(1,128)S(1)}) custom-call(bf16[128,4096]{1,0:T(8,128)(2,1)} %token_ref.1, f32[1,4096]{1,0:T(1,128)} %bitcast.24, bf16[4096,128]{1,0:T(8,128)(2,1)} %refs_2_.1, s32[2,128]{1,0:T(2,128)} %bitcast.27, f32[1,4096]{1,0:T(1,128)} %bitcast.25), custom_call_target="tpu_custom_call" | custom-call | flops 10000000000 | bytes 4194304 | tf_op jit(solution)/shard_map/gate/pallas_call | solution.py:197
  78.7 36.7 %all-to-all-done.1 = bf16[128,96,128]{2,1,0:T(8,128)(2,1)S(1)} async-done(((bf16[128,96,128]{2,1,0:T(8,128)(2,1)}), bf16[128,96,128]{2,1,0:T(8,128)(2,1)S(1)}, u32[]{:S(2)}, u32[]{:S(2)}) %all-to-all-start.1) | async-done | bytes 3145760 | tf_op jit(solution)/shard_map/all_to_all | solution.py:389
  115.4 0.0 copy-done
  115.4 0.0 copy-done.1
  115.4 1.5 %value.1 = (f32[1,128]{1,0:T(1,128)S(1)}, f32[128,128]{1,0:T(8,128)}) custom-call(bf16[384,32,128]{2,1,0:T(8,128)(2,1)S(1)} %bitcast.16, f32[8,128]{1,0:T(8,128)S(4)} %get-tuple-element.8.gates_ref.gates_smem, s32[8,128]{1,0:T(8,128)S(4)} %get-tuple-element.9.where_ref.where_smem, f32[1,128]{1,0:T(1,128)S(1)} %get-tuple-element.10.base_ref, ...), custom_call_target="tpu_custom_call" | custom-call | tf_op jit(solution)/shard_map/value/pallas_call | solution.py:327
  116.9 4.9 %all-to-all-start.2 = ((f32[128,1,128]{2,1,0:T(1,128)}), f32[128,1,128]{2,1,0:T(1,128)S(1)}, u32[]{:S(2)}, u32[]{:S(2)}) async-start(f32[128,1,128]{2,1,0:T(1,128)} %bitcast.11), calls=%async_computation.2 | async-start | bytes 131072 | tf_op jit(solution)/shard_map/all_to_all | solution.py:389
  121.8 2.8 %mix.1 = bf16[128,4096]{1,0:T(8,128)(2,1)} custom-call(bf16[384,32,128]{2,1,0:T(8,128)(2,1)S(1)} %bitcast.17, bf16[128,4096]{1,0:T(8,128)(2,1)} %token_ref.1, f32[8,128]{1,0:T(8,128)S(4)} %get-tuple-element.8.gates_ref.gates_smem, s32[8,128]{1,0:T(8,128)S(4)} %get-tuple-element.9.where_ref.where_smem), custom_call_target="tpu_custom_call" | custom-call | flops 10000000000 | bytes 6291456 | tf_op jit(solution)/shard_map/mix/pallas_call | solution.py:370
  124.6 0.5 copy.14
  125.1 6.2 %all-to-all-done.2 = f32[128,1,128]{2,1,0:T(1,128)S(1)} async-done(((f32[128,1,128]{2,1,0:T(1,128)}), f32[128,1,128]{2,1,0:T(1,128)S(1)}, u32[]{:S(2)}, u32[]{:S(2)}) %all-to-all-start.2) | async-done | bytes 65568 | tf_op jit(solution)/shard_map/all_to_all | solution.py:389
  131.4 0.7 slice_reduce_fusion
Async XLA Ops:
  69.0 5.1 %copy-start.2 = (bf16[4096]{0:T(1024)(128)(2,1)S(1)}, bf16[4096]{0:T(1024)(128)(2,1)}, u32[]{:S(2)}) copy-start(bf16[4096]{0:T(1024)(128)(2,1)} %param.17) | copy-start | bytes 24580
  69.0 46.4 %all-to-all-start.1 = ((bf16[128,96,128]{2,1,0:T(8,128)(2,1)}), bf16[128,96,128]{2,1,0:T(8,128)(2,1)S(1)}, u32[]{:S(2)}, u32[]{:S(2)}) async-start(bf16[128,96,128]{2,1,0:T(8,128)(2,1)} %bitcast.21), calls=%async_computation.1 | async-start | bytes 6291456 | tf_op jit(solution)/shard_map/all_to_all | solution.py:389
  74.7 40.7 %copy-start = (s32[128]{0:T(128)S(1)}, s32[128]{0:T(128)}, u32[]{:S(2)}) copy-start(s32[128]{0:T(128)} %param.18) | copy-start | bytes 1540
  74.7 40.7 %copy-start.1 = (f32[128]{0:T(128)S(1)}, f32[128]{0:T(128)}, u32[]{:S(2)}) copy-start(f32[128]{0:T(128)} %param.19) | copy-start | bytes 1540
  116.9 14.5 %all-to-all-start.2 = ((f32[128,1,128]{2,1,0:T(1,128)}), f32[128,1,128]{2,1,0:T(1,128)S(1)}, u32[]{:S(2)}, u32[]{:S(2)}) async-start(f32[128,1,128]{2,1,0:T(1,128)} %bitcast.11), calls=%async_computation.2 | async-start | bytes 131072 | tf_op jit(solution)/shard_map/all_to_all | solution.py:389

commit v7 on v6

--- a/solution.py
+++ b/solution.py
@@ -385,6 +385,22 @@
     )(kept(back), far(tokens), gates, where)
 
 
+def loss_kernel(sums_ref, loss_ref):
+    total = jnp.sum(sums_ref[...], axis=0, keepdims=True)
+    loss_ref[...] = total[:, 0:1] / total[:, 1:2]
+
+
+def loss_of(sums):
+    return pl.pallas_call(
+        loss_kernel,
+        in_specs=[NEAR],
+        out_specs=NEAR,
+        out_shape=jax.ShapeDtypeStruct((1, 1), F32),
+        compiler_params=params(4),
+        name="loss",
+    )(kept(sums))
+
+
 def exchange(x):
     return lax.all_to_all(x, EXPERT, split_axis=0, concat_axis=0, tiled=True)
 
@@ -419,7 +435,7 @@
     )
     everyone = exchange(sums.reshape(experts, 1, LANES)).reshape(experts, LANES)
     mixed = mix(back, tokens, gates, where)
-    return (mixed, values.reshape(count), jnp.sum(everyone[:, 0]) / jnp.sum(everyone[:, 1]))
+    return (mixed, values.reshape(count), loss_of(everyone).reshape(()))
 
 
 def solution(mesh):

time: 135 us -> 132 us (0.978)
  between operations: 3.07 us -> 0.7 us
where the time goes in v7:
time: 132 us
  blocking collectives  52.7 us (40%)
  waiting for transfers between devices  42.9 us (32%)
  Pallas kernels  24.6 us (19%)
  starting transfers between devices  10 us (8%)
    all_to_all x1, blocking collectives, exchange(): return lax.all_to_all(x, EXPERT, split_axis=0, concat_axis=0, tiled=True)  52.7 us
    all_to_all x2, waiting for transfers between devices, exchange(): return lax.all_to_all(x, EXPERT, split_axis=0, concat_axis=0, tiled=True)  42.9 us
    pallas_call x1, Pallas kernels, expert_ffn(): pl.pallas_call(ffn_kernel, in_specs=[NEAR] + [FAR] * 3, out_specs=FAR, ou...  11.5 us
    all_to_all x2, starting transfers between devices, exchange(): return lax.all_to_all(x, EXPERT, split_axis=0, concat_axis=0, tiled=True)  10 us
    pallas_call x1, Pallas kernels, route(): pl.pallas_call(route_kernel, in_specs=[FAR] * 3, out_specs=FAR, out_shape...  4.16 us
    pallas_call x1, Pallas kernels, gate(): pl.pallas_call(gate_kernel, in_specs=[FAR] * 5, out_specs=[SCALARS, SCALA...  4.02 us
    pallas_call x1, Pallas kernels, mix(): pl.pallas_call(mix_kernel, in_specs=[NEAR, FAR] + [SCALARS] * 2, out_spec...  2.83 us
  transfers between devices with their start and end apart: 2, of which 2 were waited for; matrix products, arithmetic and copies ran while one was open for 1% of the time, Pallas kernels for 5%

profile of v7, /device:TPU:1, one launch (start us, length us, event | category | flops | bytes accessed | tf_op | source)
XLA Modules:
  0.0 132.0 jit_solution(5749990877529823539)
XLA Ops:
  0.6 4.2 %route.1 = bf16[128,96,128]{2,1,0:T(8,128)(2,1)} custom-call(bf16[128,4096]{1,0:T(8,128)(2,1)} %token_ref.1, f32[1,4096]{1,0:T(1,128)} %bitcast.24, s32[2,128]{1,0:T(2,128)} %bitcast.27), custom_call_target="tpu_custom_call" | custom-call | tf_op jit(solution)/shard_map/route/pallas_call | solution.py:136
  4.8 52.7 %all_to_all.15 = bf16[128,96,128]{2,1,0:T(8,128)(2,1)S(1)} all-to-all(bf16[128,96,128]{2,1,0:T(8,128)(2,1)} %route.1), channel_id=1, replica_groups=mesh['expert_0'=4,'expert_1'=4,'expert_2'=4,'expert_3'=2] {'expert_0','e..., dimensions={0} | all-to-all | bytes 6291456 | tf_op jit(solution)/shard_map/all_to_all | solution.py:405
  57.5 11.5 %ffn.1 = bf16[384,32,128]{2,1,0:T(8,128)(2,1)} custom-call(bf16[384,32,128]{2,1,0:T(8,128)(2,1)S(1)} %bitcast.19, bf16[1,4096,768]{2,1,0:T(8,128)(2,1)} %gate_ref.1, bf16[1,4096,768]{2,1,0:T(8,128)(2,1)} %up_ref.1, bf16[1,768,4096]{2,1,0:T(8,128)(2,1)} %down_ref.1), custom_call_target="tpu_custom_call" | custom-call | flops 7247757312 | bytes 25165824 | tf_op jit(solution)/shard_map/ffn/pallas_call | solution.py:276
  69.0 0.0 copy-start.2
  69.0 5.1 %all-to-all-start.1 = ((bf16[128,96,128]{2,1,0:T(8,128)(2,1)}), bf16[128,96,128]{2,1,0:T(8,128)(2,1)S(1)}, u32[]{:S(2)}, u32[]{:S(2)}) async-start(bf16[128,96,128]{2,1,0:T(8,128)(2,1)} %bitcast.23), calls=%async_computation.1 | async-start | bytes 6291456 | tf_op jit(solution)/shard_map/all_to_all | solution.py:405
  74.1 0.0 copy-done.2
  74.1 0.6 convert_bitcast_fusion
  74.7 0.0 copy-start
  74.7 0.0 copy-start.1
  74.7 4.0 %gate.1 = (f32[8,128]{1,0:T(8,128)S(4)}, s32[8,128]{1,0:T(8,128)S(4)}, f32[1,128]{1,0:T(1,128)S(1)}) custom-call(bf16[128,4096]{1,0:T(8,128)(2,1)} %token_ref.1, f32[1,4096]{1,0:T(1,128)} %bitcast.25, bf16[4096,128]{1,0:T(8,128)(2,1)} %refs_2_.1, s32[2,128]{1,0:T(2,128)} %bitcast.28, f32[1,4096]{1,0:T(1,128)} %bitcast.26), custom_call_target="tpu_custom_call" | custom-call | flops 10000000000 | bytes 4194304 | tf_op jit(solution)/shard_map/gate/pallas_call | solution.py:197
  78.7 36.7 %all-to-all-done.1 = bf16[128,96,128]{2,1,0:T(8,128)(2,1)S(1)} async-done(((bf16[128,96,128]{2,1,0:T(8,128)(2,1)}), bf16[128,96,128]{2,1,0:T(8,128)(2,1)S(1)}, u32[]{:S(2)}, u32[]{:S(2)}) %all-to-all-start.1) | async-done | bytes 3145760 | tf_op jit(solution)/shard_map/all_to_all | solution.py:405
  115.4 0.0 copy-done
  115.4 0.0 copy-done.1
  115.4 1.5 %value.1 = (f32[1,128]{1,0:T(1,128)S(1)}, f32[128,128]{1,0:T(8,128)}) custom-call(bf16[384,32,128]{2,1,0:T(8,128)(2,1)S(1)} %bitcast.17, f32[8,128]{1,0:T(8,128)S(4)} %get-tuple-element.8.gates_ref.gates_smem, s32[8,128]{1,0:T(8,128)S(4)} %get-tuple-element.9.where_ref.where_smem, f32[1,128]{1,0:T(1,128)S(1)} %get-tuple-element.10.base_ref, ...), custom_call_target="tpu_custom_call" | custom-call | tf_op jit(solution)/shard_map/value/pallas_call | solution.py:327
  116.9 5.0 %all-to-all-start.2 = ((f32[128,1,128]{2,1,0:T(1,128)}), f32[128,1,128]{2,1,0:T(1,128)S(1)}, u32[]{:S(2)}, u32[]{:S(2)}) async-start(f32[128,1,128]{2,1,0:T(1,128)} %bitcast.11), calls=%async_computation.2 | async-start | bytes 131072 | tf_op jit(solution)/shard_map/all_to_all | solution.py:405
  121.8 2.8 %mix.1 = bf16[128,4096]{1,0:T(8,128)(2,1)} custom-call(bf16[384,32,128]{2,1,0:T(8,128)(2,1)S(1)} %bitcast.18, bf16[128,4096]{1,0:T(8,128)(2,1)} %token_ref.1, f32[8,128]{1,0:T(8,128)S(4)} %get-tuple-element.8.gates_ref.gates_smem, s32[8,128]{1,0:T(8,128)S(4)} %get-tuple-element.9.where_ref.where_smem), custom_call_target="tpu_custom_call" | custom-call | flops 10000000000 | bytes 6291456 | tf_op jit(solution)/shard_map/mix/pallas_call | solution.py:370
  124.6 0.5 copy.14
  125.2 6.2 %all-to-all-done.2 = f32[128,1,128]{2,1,0:T(1,128)S(1)} async-done(((f32[128,1,128]{2,1,0:T(1,128)}), f32[128,1,128]{2,1,0:T(1,128)S(1)}, u32[]{:S(2)}, u32[]{:S(2)}) %all-to-all-start.2) | async-done | bytes 65568 | tf_op jit(solution)/shard_map/all_to_all | solution.py:405
  131.4 0.6 loss.1
Async XLA Ops:
  69.0 5.1 %copy-start.2 = (bf16[4096]{0:T(1024)(128)(2,1)S(1)}, bf16[4096]{0:T(1024)(128)(2,1)}, u32[]{:S(2)}) copy-start(bf16[4096]{0:T(1024)(128)(2,1)} %param.17) | copy-start | bytes 24580
  69.0 46.4 %all-to-all-start.1 = ((bf16[128,96,128]{2,1,0:T(8,128)(2,1)}), bf16[128,96,128]{2,1,0:T(8,128)(2,1)S(1)}, u32[]{:S(2)}, u32[]{:S(2)}) async-start(bf16[128,96,128]{2,1,0:T(8,128)(2,1)} %bitcast.23), calls=%async_computation.1 | async-start | bytes 6291456 | tf_op jit(solution)/shard_map/all_to_all | solution.py:405
  74.7 40.7 %copy-start = (s32[128]{0:T(128)S(1)}, s32[128]{0:T(128)}, u32[]{:S(2)}) copy-start(s32[128]{0:T(128)} %param.18) | copy-start | bytes 1540
  74.7 40.7 %copy-start.1 = (f32[128]{0:T(128)S(1)}, f32[128]{0:T(128)}, u32[]{:S(2)}) copy-start(f32[128]{0:T(128)} %param.19) | copy-start | bytes 1540
  116.9 14.5 %all-to-all-start.2 = ((f32[128,1,128]{2,1,0:T(1,128)}), f32[128,1,128]{2,1,0:T(1,128)S(1)}, u32[]{:S(2)}, u32[]{:S(2)}) async-start(f32[128,1,128]{2,1,0:T(1,128)} %bitcast.11), calls=%async_computation.2 | async-start | bytes 131072 | tf_op jit(solution)/shard_map/all_to_all | solution.py:405

commit v8 on v7

--- a/solution.py
+++ b/solution.py
@@ -67,6 +67,14 @@
     before = jnp.where(iota((count, count), 0) < iota((count, count), 1), 1.0, 0.0).astype(BF16)
     rank = jnp.dot(named, before, preferred_element_type=F32)
     return hits, rank
+
+
+def place_of(expert):
+    return (expert & 1) * 64 + ((expert >> 1) & 3) * 16 + ((expert >> 3) & 3) * 4 + (expert >> 5)
+
+
+def expert_at(place):
+    return (place & 3) * 32 + ((place >> 2) & 3) * 8 + ((place >> 4) & 3) * 2 + (place >> 6)
 
 
 def norm(wide, gain):
@@ -119,7 +127,7 @@
             for i in range(4):
                 e = c * chunk + step * 4 + i
                 for s in range(SLOTS):
-                    piece_ref[e, s * parts:(s + 1) * parts] = tall_ref[index_smem[s, e]]
+                    piece_ref[e, s * parts:(s + 1) * parts] = tall_ref[index_smem[s, expert_at(e)]]
             return carry
 
         lax.fori_loop(0, chunk // 4, send, 0)
@@ -183,7 +191,7 @@
     gates_ref[...] = jnp.zeros(gates_ref.shape, F32)
     for k in range(2):
         slot = jnp.sum(jnp.where(hits[k], rank, 0.0), axis=0, keepdims=True).astype(I32)
-        where_ref[k:k + 1, :] = ids_ref[k:k + 1, :] * SLOTS + slot
+        where_ref[k:k + 1, :] = place_of(ids_ref[k:k + 1, :]) * SLOTS + slot
         scores.append(jnp.sum(jnp.where(hits[k], logits, 0.0), axis=0, keepdims=True))
     gates_ref[0:1, :] = jax.nn.sigmoid(scores[0] - scores[1])
     gates_ref[1:2, :] = jax.nn.sigmoid(scores[1] - scores[0])
@@ -402,7 +410,7 @@
 
 
 def exchange(x):
-    return lax.all_to_all(x, EXPERT, split_axis=0, concat_axis=0, tiled=True)
+    return lax.all_to_all(x, EXPERT[::-1], split_axis=0, concat_axis=0, tiled=True)
 
 
 def body(

time: 132 us -> 135 us (1.023)
  starting transfers between devices: 10 us -> 14.2 us
    all_to_all x2, starting transfers between devices: 10 us -> 14.2 us  [exchange(): lax.all_to_all(x, EXPERT[::-1], split_axis=0, concat_axis=0, tiled=True)]
where the time goes in v8:
time: 135 us; the launch traced here: 134 us
  blocking collectives  51.6 us (38%)
  waiting for transfers between devices  41.6 us (31%)
  Pallas kernels  24.8 us (18%)
  starting transfers between devices  14.2 us (11%)
    all_to_all x1, blocking collectives, exchange(): lax.all_to_all(x, EXPERT[::-1], split_axis=0, concat_axis=0, tiled=True)  51.6 us
    all_to_all x2, waiting for transfers between devices, exchange(): lax.all_to_all(x, EXPERT[::-1], split_axis=0, concat_axis=0, tiled=True)  41.6 us
    all_to_all x2, starting transfers between devices, exchange(): lax.all_to_all(x, EXPERT[::-1], split_axis=0, concat_axis=0, tiled=True)  14.2 us
    pallas_call x1, Pallas kernels, expert_ffn(): pl.pallas_call(ffn_kernel, in_specs=[NEAR] + [FAR] * 3, out_specs=FAR, ou...  11.5 us
    pallas_call x1, Pallas kernels, route(): pl.pallas_call(route_kernel, in_specs=[FAR] * 3, out_specs=FAR, out_shape...  4.36 us
    pallas_call x1, Pallas kernels, gate(): pl.pallas_call(gate_kernel, in_specs=[FAR] * 5, out_specs=[SCALARS, SCALA...  4.02 us
    pallas_call x1, Pallas kernels, mix(): pl.pallas_call(mix_kernel, in_specs=[NEAR, FAR] + [SCALARS] * 2, out_spec...  2.83 us
  transfers between devices with their start and end apart: 2, of which 2 were waited for; matrix products, arithmetic and copies ran while one was open for 1% of the time, Pallas kernels for 5%

profile of v8, /device:TPU:1, one launch (start us, length us, event | category | flops | bytes accessed | tf_op | source)
XLA Modules:
  0.0 134.1 jit_solution(12439002762492881475)
XLA Ops:
  0.6 4.4 %route.1 = bf16[128,96,128]{2,1,0:T(8,128)(2,1)} custom-call(bf16[128,4096]{1,0:T(8,128)(2,1)} %token_ref.1, f32[1,4096]{1,0:T(1,128)} %bitcast.24, s32[2,128]{1,0:T(2,128)} %bitcast.27), custom_call_target="tpu_custom_call" | custom-call | tf_op jit(solution)/shard_map/route/pallas_call | solution.py:144
  5.0 51.6 %all_to_all.15 = bf16[128,96,128]{2,1,0:T(8,128)(2,1)S(1)} all-to-all(bf16[128,96,128]{2,1,0:T(8,128)(2,1)} %route.1), channel_id=1, replica_groups=mesh['expert_0'=4,'expert_1'=4,'expert_2'=4,'expert_3'=2] {'expert_3','e..., dimensions={0} | all-to-all | bytes 6291456 | tf_op jit(solution)/shard_map/all_to_all | solution.py:413
  56.6 11.5 %ffn.1 = bf16[384,32,128]{2,1,0:T(8,128)(2,1)} custom-call(bf16[384,32,128]{2,1,0:T(8,128)(2,1)S(1)} %bitcast.19, bf16[1,4096,768]{2,1,0:T(8,128)(2,1)} %gate_ref.1, bf16[1,4096,768]{2,1,0:T(8,128)(2,1)} %up_ref.1, bf16[1,768,4096]{2,1,0:T(8,128)(2,1)} %down_ref.1), custom_call_target="tpu_custom_call" | custom-call | flops 7247757312 | bytes 25165824 | tf_op jit(solution)/shard_map/ffn/pallas_call | solution.py:284
  68.2 0.0 copy-start.2
  68.2 7.1 %all-to-all-start.1 = ((bf16[128,96,128]{2,1,0:T(8,128)(2,1)}), bf16[128,96,128]{2,1,0:T(8,128)(2,1)S(1)}, u32[]{:S(2)}, u32[]{:S(2)}) async-start(bf16[128,96,128]{2,1,0:T(8,128)(2,1)} %bitcast.23), calls=%async_computation.1 | async-start | bytes 6291456 | tf_op jit(solution)/shard_map/all_to_all | solution.py:413
  75.3 0.0 copy-done.2
  75.3 0.6 convert_bitcast_fusion
  75.9 0.0 copy-start
  75.9 0.0 copy-start.1
  75.9 4.0 %gate.1 = (f32[8,128]{1,0:T(8,128)S(4)}, s32[8,128]{1,0:T(8,128)S(4)}, f32[1,128]{1,0:T(1,128)S(1)}) custom-call(bf16[128,4096]{1,0:T(8,128)(2,1)} %token_ref.1, f32[1,4096]{1,0:T(1,128)} %bitcast.25, bf16[4096,128]{1,0:T(8,128)(2,1)} %refs_2_.1, s32[2,128]{1,0:T(2,128)} %bitcast.28, f32[1,4096]{1,0:T(1,128)} %bitcast.26), custom_call_target="tpu_custom_call" | custom-call | flops 10000000000 | bytes 4194304 | tf_op jit(solution)/shard_map/gate/pallas_call | solution.py:205
  79.9 35.5 %all-to-all-done.1 = bf16[128,96,128]{2,1,0:T(8,128)(2,1)S(1)} async-done(((bf16[128,96,128]{2,1,0:T(8,128)(2,1)}), bf16[128,96,128]{2,1,0:T(8,128)(2,1)S(1)}, u32[]{:S(2)}, u32[]{:S(2)}) %all-to-all-start.1) | async-done | bytes 3145760 | tf_op jit(solution)/shard_map/all_to_all | solution.py:413
  115.4 0.0 copy-done
  115.4 0.0 copy-done.1
  115.4 1.5 %value.1 = (f32[1,128]{1,0:T(1,128)S(1)}, f32[128,128]{1,0:T(8,128)}) custom-call(bf16[384,32,128]{2,1,0:T(8,128)(2,1)S(1)} %bitcast.17, f32[8,128]{1,0:T(8,128)S(4)} %get-tuple-element.8.gates_ref.gates_smem, s32[8,128]{1,0:T(8,128)S(4)} %get-tuple-element.9.where_ref.where_smem, f32[1,128]{1,0:T(1,128)S(1)} %get-tuple-element.10.base_ref, ...), custom_call_target="tpu_custom_call" | custom-call | tf_op jit(solution)/shard_map/value/pallas_call | solution.py:335
  116.9 7.1 %all-to-all-start.2 = ((f32[128,1,128]{2,1,0:T(1,128)}), f32[128,1,128]{2,1,0:T(1,128)S(1)}, u32[]{:S(2)}, u32[]{:S(2)}) async-start(f32[128,1,128]{2,1,0:T(1,128)} %bitcast.11), calls=%async_computation.2 | async-start | bytes 131072 | tf_op jit(solution)/shard_map/all_to_all | solution.py:413
  124.1 2.8 %mix.1 = bf16[128,4096]{1,0:T(8,128)(2,1)} custom-call(bf16[384,32,128]{2,1,0:T(8,128)(2,1)S(1)} %bitcast.18, bf16[128,4096]{1,0:T(8,128)(2,1)} %token_ref.1, f32[8,128]{1,0:T(8,128)S(4)} %get-tuple-element.8.gates_ref.gates_smem, s32[8,128]{1,0:T(8,128)S(4)} %get-tuple-element.9.where_ref.where_smem), custom_call_target="tpu_custom_call" | custom-call | flops 10000000000 | bytes 6291456 | tf_op jit(solution)/shard_map/mix/pallas_call | solution.py:378
  126.9 0.5 copy.14
  127.4 6.1 %all-to-all-done.2 = f32[128,1,128]{2,1,0:T(1,128)S(1)} async-done(((f32[128,1,128]{2,1,0:T(1,128)}), f32[128,1,128]{2,1,0:T(1,128)S(1)}, u32[]{:S(2)}, u32[]{:S(2)}) %all-to-all-start.2) | async-done | bytes 65568 | tf_op jit(solution)/shard_map/all_to_all | solution.py:413
  133.5 0.6 loss.1
Async XLA Ops:
  68.2 7.1 %copy-start.2 = (bf16[4096]{0:T(1024)(128)(2,1)S(1)}, bf16[4096]{0:T(1024)(128)(2,1)}, u32[]{:S(2)}) copy-start(bf16[4096]{0:T(1024)(128)(2,1)} %param.17) | copy-start | bytes 24580
  68.2 47.3 %all-to-all-start.1 = ((bf16[128,96,128]{2,1,0:T(8,128)(2,1)}), bf16[128,96,128]{2,1,0:T(8,128)(2,1)S(1)}, u32[]{:S(2)}, u32[]{:S(2)}) async-start(bf16[128,96,128]{2,1,0:T(8,128)(2,1)} %bitcast.23), calls=%async_computation.1 | async-start | bytes 6291456 | tf_op jit(solution)/shard_map/all_to_all | solution.py:413
  75.9 39.5 %copy-start = (s32[128]{0:T(128)S(1)}, s32[128]{0:T(128)}, u32[]{:S(2)}) copy-start(s32[128]{0:T(128)} %param.18) | copy-start | bytes 1540
  75.9 39.5 %copy-start.1 = (f32[128]{0:T(128)S(1)}, f32[128]{0:T(128)}, u32[]{:S(2)}) copy-start(f32[128]{0:T(128)} %param.19) | copy-start | bytes 1540
  116.9 16.6 %all-to-all-start.2 = ((f32[128,1,128]{2,1,0:T(1,128)}), f32[128,1,128]{2,1,0:T(1,128)S(1)}, u32[]{:S(2)}, u32[]{:S(2)}) async-start(f32[128,1,128]{2,1,0:T(1,128)} %bitcast.11), calls=%async_computation.2 | async-start | bytes 131072 | tf_op jit(solution)/shard_map/all_to_all | solution.py:413
